TPU v7x, 128 devices: a whole 4x4x4 slice. The times are simulated.
128 devices in a mesh: elem: 128 (over z, y, x, core).
Axes of the slice: x: 4, y: 4, z: 4, core: 2. Of those that a mesh axis runs over, the one named last changes fastest.
Arguments:
- tracers: float32 [2048, 4, 16, 128], P('elem'), may hold values from -6 to 6
- sources: float32 [2048, 4, 16, 128], P('elem'), may hold values from -3 to 3
- weights: float32 [2048, 4, 256], P('elem'), may hold values from -0.3 to 0.425
- dep_owner: int32 [2048, 4, 16], P('elem'), may hold values from 0 to 127, as said below
- dep_slot: int32 [2048, 4, 16], P('elem'), may hold values from 0 to 15, as said below
- nbr_elem: int32 [2048, 4], P('elem'), may hold values from 0 to 2047, as said below
- nbr_edge: int32 [2048, 4], P('elem'), may hold values from 0 to 3, as said below
- metric: float32 [2048, 2, 16], P('elem'), may hold values from 0.5 to 2
Outputs:
- settled: float32 [2048, 4, 16, 128], P('elem')
Inputs may be any that keep to these rules, and one draw needn't show every extreme that they name: `dep_owner`: the departure element of a target point is its own element or one of its four edge neighbours, so its owner is the point's own device or the one before or after it, cyclically. Of one device's target points at most 1024 have departure elements on the next device and at most 1024 on the previous one; each bound is reached on some device in every draw. `dep_slot`: together with dep_owner it names the departure element. `nbr_elem`: global index is owner times 16 plus position. Edges are listed counterclockwise; the relation is symmetric and no element is its own neighbour. Every neighbour lies on the same device or the one before or after it, cyclically; exactly 16 edges of one device's elements face the next device and exactly 16 the previous one. `nbr_edge`: the neighbour's entry for that edge points back to the element and edge.
All inputs are finite; a program needn't handle non-finite values.
Results may differ from a plain program's by a relative error of at most 0.0003.
Values sent between devices are 32-bit elements; how exact they have to be, the bound alone decides.
A program may use at most 128 MiB of HBM per device.

v0:
```python
import jax
import jax.numpy as jnp
import numpy as np
from jax import lax
from jax.sharding import PartitionSpec as P

VISCOSITY = 0.002
HIGH = lax.Precision.HIGHEST


def extended_2(x, sides, width):
    for axis, dim in sides:
        peers, length = (lax.axis_size(axis), x.shape[dim])
        up = [(i, (i + 1) % peers) for i in range(peers)]
        down = [(j, i) for i, j in up]
        last = lax.slice_in_dim(x, length - width, length, axis=dim)
        first = lax.slice_in_dim(x, 0, width, axis=dim)
        before = lax.ppermute(last, axis, up)
        after = lax.ppermute(first, axis, down)
        x = jnp.concatenate([before, x, after], axis=dim)
    return x


def gll_tables():
    gll_nodes = np.array([-1.0, -np.sqrt(0.2), np.sqrt(0.2), 1.0])
    node_count = gll_nodes.shape[0]
    bary_weights = np.array(
        [
            1.0 / np.prod([gll_nodes[j] - gll_nodes[m] for m in range(node_count) if m != j])
            for j in range(node_count)
        ]
    )
    derivative = np.zeros((node_count, node_count))
    for i in range(node_count):
        for j in range(node_count):
            if i != j:
                derivative[i, j] = bary_weights[j] / bary_weights[i] / (gll_nodes[i] - gll_nodes[j])
        derivative[i, i] = -np.sum(derivative[i])
    identity = np.eye(node_count)
    along_a = np.kron(derivative, identity)
    along_b = np.kron(identity, derivative)
    edge_points = np.array(
        [
            [4 * k for k in range(4)],
            [12 + k for k in range(4)],
            [4 * (3 - k) + 3 for k in range(4)],
            [3 - k for k in range(4)],
        ],
        dtype=np.int32,
    )
    spread = np.zeros((4, 4, 16))
    for s in range(4):
        for k in range(4):
            spread[s, k, edge_points[s, k]] = 1.0
    counts = 1.0 + spread.sum(axis=(0, 1))
    return (along_a, along_b, edge_points, spread, counts)


def candidate_mix(table, cand_index, cand_global, dep_global, weights):
    element_count = dep_global.shape[0]
    level_count = dep_global.shape[1]
    points = dep_global.shape[2]
    candidates = table[cand_index]
    shaped = weights.reshape(element_count, level_count, points, points)
    mixed = jnp.einsum("elpj,ecljq->eclpq", shaped, candidates, precision=HIGH)
    matched = (dep_global[..., None] == cand_global[:, None, None, :]).astype(jnp.float32)
    return jnp.einsum("elpc,eclpq->elpq", matched, mixed, precision=HIGH)


def local_laplacian(field_in, metric, tables):
    along_a = jnp.asarray(tables[0], field_in.dtype)
    along_b = jnp.asarray(tables[1], field_in.dtype)
    grad_a = jnp.einsum("pm,elmq->elpq", along_a, field_in, precision=HIGH)
    grad_b = jnp.einsum("pm,elmq->elpq", along_b, field_in, precision=HIGH)
    flux_a = metric[:, 0][:, None, :, None] * grad_a
    flux_b = metric[:, 1][:, None, :, None] * grad_b
    return jnp.einsum("pm,elmq->elpq", along_a, flux_a, precision=HIGH) + jnp.einsum(
        "pm,elmq->elpq", along_b, flux_b, precision=HIGH
    )


def partner_edges(gathered, facing_edge, tables):
    reversed_points = jnp.asarray(tables[2][:, ::-1].copy(), jnp.int32)
    pick = (facing_edge[..., None] == jnp.arange(4, dtype=jnp.int32)).astype(jnp.int32)
    wanted = jnp.sum(pick[..., None] * reversed_points, axis=2)
    select = (wanted[..., None] == jnp.arange(gathered.shape[3], dtype=jnp.int32)).astype(
        gathered.dtype
    )
    return jnp.einsum("eskp,eslpq->eslkq", select, gathered, precision=HIGH)


def close_edges(field_in, received, tables):
    spread = jnp.asarray(tables[3], field_in.dtype)
    counts = jnp.asarray(tables[4], field_in.dtype)
    added = jnp.einsum("skp,eslkq->elpq", spread, received, precision=HIGH)
    return (field_in + added) / counts[None, None, :, None]


def advect(field_in, dep_owner, dep_slot, weights, nbr_elem, devices, myself):
    local_count = field_in.shape[0]
    own_local = jnp.arange(local_count, dtype=jnp.int32)
    own_global = myself * local_count + own_local
    cand_global = jnp.concatenate([own_global[:, None], nbr_elem], axis=1)
    dep_global = dep_owner * local_count + dep_slot
    owner_of = nbr_elem // local_count
    slot_of = nbr_elem % local_count
    extended = extended_2(field_in, (("elem", 0),), local_count)
    offset = (owner_of - myself + 1 + devices) % devices
    cand_index = jnp.concatenate(
        [(own_local + local_count)[:, None], offset * local_count + slot_of], axis=1
    )
    return candidate_mix(extended, cand_index, cand_global, dep_global, weights)


def edge_close(field_in, nbr_elem, nbr_edge, devices, myself, tables):
    local_count = field_in.shape[0]
    owner_of = nbr_elem // local_count
    slot_of = nbr_elem % local_count
    extended = extended_2(field_in, (("elem", 0),), local_count)
    offset = (owner_of - myself + 1 + devices) % devices
    received = partner_edges(extended[offset * local_count + slot_of], nbr_edge, tables)
    return close_edges(field_in, received, tables)


def local(tracers, sources, weights, dep_owner, dep_slot, nbr_elem, nbr_edge, metric):
    tables = gll_tables()
    devices = lax.axis_size("elem")
    myself = lax.axis_index("elem")
    first = advect(tracers, dep_owner, dep_slot, weights, nbr_elem, devices, myself) + sources
    second = advect(first, dep_owner, dep_slot, weights, nbr_elem, devices, myself) + sources
    lap_once = edge_close(
        local_laplacian(second, metric, tables), nbr_elem, nbr_edge, devices, myself, tables
    )
    lap_twice = edge_close(
        local_laplacian(lap_once, metric, tables), nbr_elem, nbr_edge, devices, myself, tables
    )
    return second - VISCOSITY * lap_twice


def solution(mesh):
    placed = (
        P("elem", None, None, None),
        P("elem", None, None, None),
        P("elem", None, None),
        P("elem", None, None),
        P("elem", None, None),
        P("elem", None),
        P("elem", None),
        P("elem", None, None),
    )
    return jax.shard_map(
        local, mesh=mesh, in_specs=placed, out_specs=P("elem", None, None, None), check_vma=False
    )
```

profile of v0, /device:TPU:0, one launch (start us, length us, event | category | flops | bytes accessed | tf_op | source)
XLA Modules:
  0.0 98.8 jit_solution(11584058819676764198)
XLA Ops:
  0.0 0.0 collective-permute-start
  0.0 8.2 %collective-permute-start.1 = (f32[16,4,16,128]{3,2,1,0:T(8,128)}, f32[16,4,16,128]{3,2,1,0:T(8,128)S(1)}, u32[]{:S(2)}, u32[]{:S(2)}) collective-permute-start(f32[16,4,16,128]{3,2,1,0:T(8,128)} %param.18), channel_id=1, source_target_pairs={{1,0},{2,1},{3,2},{4,3},{5,4},{6,5},{7,6},{8,7},{9,8},{10,9},{11,1... | collective-permute-start | bytes 1572872 | tf_op jit(solution)/shard_map/ppermute | solution.py:19
  8.2 0.7 compare_select_fusion.1
  9.0 0.1 copy.31
  9.0 0.1 reshape.104
  9.1 1.0 %reshape.140 = f32[16,4,16,16,1]{3,2,1,0,4:T(8,128)S(1)} reshape(f32[16,4,256]{2,1,0:T(4,128)} %param.20) | data formatting | bytes 131072 | tf_op jit(solution)/shard_map/reshape | solution.py:64
  10.2 0.7 pad_add_fusion
  10.9 0.1 copy.29
  11.0 0.8 multiply_add_fusion
  11.8 0.2 compare_bitcast_fusion
  12.0 3.3 %collective-permute-done = f32[16,4,16,128]{3,2,1,0:T(8,128)S(1)} collective-permute-done((f32[16,4,16,128]{3,2,1,0:T(8,128)}, f32[16,4,16,128]{3,2,1,0:T(8,128)S(1)}, u32[]{:S(2)}, u32[]{:S(2)}) %collective-permute-start) | collective-permute-done | bytes 524320 | tf_op jit(solution)/shard_map/ppermute | solution.py:18
  15.3 0.0 collective-permute-done.1
  15.3 1.2 %pad_maximum_fusion = f32[48,4,16,128]{3,2,1,0:T(8,128)S(1)} fusion(f32[16,4,16,128]{3,2,1,0:T(8,128)S(1)} %collective-permute-done.1, f32[16,4,16,128]{3,2,1,0:T(8,128)} %param.18, f32[16,4,16,128]{3,2,1,0:T(8,128)S(1)} %collective-permute-done), kind=kLoop, calls=%fused_computation.16 | loop fusion | flops 786432 | bytes 3145728 | tf_op jit(solution)/shard_map/concatenate | solution.py:20
  16.5 2.2 %gather_fusion = f32[80,4,16,128]{3,2,1,0:T(8,128)} fusion(f32[48,4,16,128]{3,2,1,0:T(8,128)S(1)} %pad_maximum_fusion, s32[1024]{0:T(1024)S(1)} %pad_clamp_fusion.1), kind=kCustom, calls=%fused_computation | custom fusion | bytes 5243200 | tf_op jit(solution)/shard_map/gather | solution.py:63
  18.7 4.1 %fusion.10 = f32[16,5,4,16,128]{4,3,1,2,0:T(8,128)S(1)} fusion(f32[16,5,4,16,128]{4,3,2,1,0:T(8,128)} %bitcast.110, f32[16,4,16,16,1]{3,2,1,0,4:T(8,128)S(1)} %reshape.140), kind=kOutput, calls=%fused_computation.14 | convolution fusion | flops 125829120 | bytes 5308416 | tf_op jit(solution)/shard_map/elpj,ecljq->eclpq/dot_general | solution.py:65
  22.8 0.0 copy-start
  22.8 0.0 copy-start.4
  22.9 4.6 %fusion.2 = f32[16,4,16,1,128]{4,3,2,1,0:T(1,128)S(1)} fusion(f32[16,5,4,16,128]{4,3,1,2,0:T(8,128)S(1)} %fusion.10, pred[16,4,16,5,1]{3,2,1,0,4:T(8,128)(4,1)S(1)} %compare_bitcast_fusion), kind=kOutput, calls=%fused_computation.6 | convolution fusion | flops 7864320 | bytes 3150848 | tf_op jit(solution)/shard_map/elpc,eclpq->elpq/dot_general | solution.py:67
  27.4 0.0 copy-done
  27.4 0.1 add.134
  27.5 0.1 collective-permute-start.2
  27.6 7.4 %collective-permute-start.3 = (f32[16,4,16,128]{3,2,1,0:T(8,128)S(1)}, f32[16,4,16,128]{3,2,1,0:T(8,128)S(1)}, u32[]{:S(2)}, u32[]{:S(2)}) collective-permute-start(f32[16,4,16,128]{3,2,1,0:T(8,128)S(1)} %add.134), channel_id=1, source_target_pairs={{1,0},{2,1},{3,2},{4,3},{5,4},{6,5},{7,6},{8,7},{9,8},{10,9},{11,1... | collective-permute-start | bytes 1572872 | tf_op jit(solution)/shard_map/ppermute | solution.py:19
  35.0 0.0 copy-done.4
  35.0 6.6 %collective-permute-done.2 = f32[16,4,16,128]{3,2,1,0:T(8,128)S(1)} collective-permute-done((f32[16,4,16,128]{3,2,1,0:T(8,128)S(1)}, f32[16,4,16,128]{3,2,1,0:T(8,128)S(1)}, u32[]{:S(2)}, u32[]{:S(2)}) %collective-permute-start.2) | collective-permute-done | bytes 524320 | tf_op jit(solution)/shard_map/ppermute | solution.py:18
  41.6 0.1 collective-permute-done.3
  41.7 0.1 pad_maximum_fusion.1
  41.8 2.2 %gather_fusion.1 = f32[80,4,16,128]{3,2,1,0:T(8,128)} fusion(f32[48,4,16,128]{3,2,1,0:T(8,128)S(1)} %pad_maximum_fusion.1, s32[1024]{0:T(1024)S(1)} %pad_clamp_fusion.1), kind=kCustom, calls=%fused_computation.1 | custom fusion | bytes 5243200 | tf_op jit(solution)/shard_map/gather | solution.py:63
  44.0 4.1 %fusion.13 = f32[16,5,4,16,128]{4,3,1,2,0:T(8,128)S(1)} fusion(f32[16,5,4,16,128]{4,3,2,1,0:T(8,128)} %bitcast.109, f32[16,4,16,16,1]{3,2,1,0,4:T(8,128)S(1)} %reshape.140), kind=kOutput, calls=%fused_computation.15 | convolution fusion | flops 125829120 | bytes 5308416 | tf_op jit(solution)/shard_map/elpj,ecljq->eclpq/dot_general | solution.py:65
  48.2 0.0 copy-start.2
  48.2 4.6 %fusion = f32[16,4,16,1,128]{4,3,2,1,0:T(1,128)S(1)} fusion(f32[16,5,4,16,128]{4,3,1,2,0:T(8,128)S(1)} %fusion.13, pred[16,4,16,5,1]{3,2,1,0,4:T(8,128)(4,1)S(1)} %compare_bitcast_fusion), kind=kOutput, calls=%fused_computation.4 | convolution fusion | flops 7864320 | bytes 3150848 | tf_op jit(solution)/shard_map/elpc,eclpq->elpq/dot_general | solution.py:67
  52.8 0.0 copy-start.1
  52.8 0.1 add.135
  52.9 0.6 fusion.21
  53.4 0.0 copy-start.6
  53.4 0.0 copy-start.7
  53.5 0.6 fusion.46
  54.0 0.0 copy-done.1
  54.0 0.6 fusion.20
  54.6 0.6 fusion.19
  55.2 0.1 collective-permute-start.4
  55.3 7.6 %collective-permute-start.5 = (f32[16,4,16,128]{3,2,1,0:T(8,128)S(1)}, f32[16,4,16,128]{3,2,1,0:T(8,128)}, u32[]{:S(2)}, u32[]{:S(2)}) collective-permute-start(f32[16,4,16,128]{3,2,1,0:T(8,128)S(1)} %fusion.19), channel_id=1, source_target_pairs={{1,0},{2,1},{3,2},{4,3},{5,4},{6,5},{7,6},{8,7},{9,8},{10,9},{11,1... | collective-permute-start | bytes 1572872 | tf_op jit(solution)/shard_map/ppermute | solution.py:19
  62.9 0.1 copy.34
  63.0 0.1 reshape.120
  63.1 0.0 copy-done.7
  63.1 0.1 multiply_reduce_fusion
  63.2 0.1 copy.35
  63.3 6.2 %collective-permute-done.4 = f32[16,4,16,128]{3,2,1,0:T(8,128)S(1)} collective-permute-done((f32[16,4,16,128]{3,2,1,0:T(8,128)S(1)}, f32[16,4,16,128]{3,2,1,0:T(8,128)S(1)}, u32[]{:S(2)}, u32[]{:S(2)}) %collective-permute-start.4) | collective-permute-done | bytes 524320 | tf_op jit(solution)/shard_map/ppermute | solution.py:18
  69.5 0.1 collective-permute-done.5
  69.6 1.2 %pad_maximum_fusion.2 = f32[48,4,16,128]{3,2,1,0:T(8,128)S(1)} fusion(f32[16,4,16,128]{3,2,1,0:T(8,128)} %collective-permute-done.5, f32[16,4,16,128]{3,2,1,0:T(8,128)S(1)} %fusion.19, f32[16,4,16,128]{3,2,1,0:T(8,128)S(1)} %collective-permute-done.4), kind=kLoop, calls=%fused_computation.18 | loop fusion | flops 786432 | bytes 3145728 | tf_op jit(solution)/shard_map/concatenate | solution.py:20
  70.8 2.0 %gather_fusion.2 = f32[64,4,16,128]{3,2,1,0:T(8,128)} fusion(f32[48,4,16,128]{3,2,1,0:T(8,128)S(1)} %pad_maximum_fusion.2, s32[1024]{0:T(1024)S(1)} %pad_clamp_fusion), kind=kCustom, calls=%fused_computation.2 | custom fusion | bytes 4194560 | tf_op jit(solution)/shard_map/gather | solution.py:121
  72.8 2.5 %convolution_bitcast_fusion.1 = f32[16,4,4,4,128]{4,3,2,1,0:T(4,128)S(1)} fusion(f32[16,4,4,16,128]{4,3,2,1,0:T(8,128)} %bitcast.112, s32[16,4,4]{2,1,0:T(4,128)S(1)} %copy.35), kind=kOutput, calls=%fused_computation.21 | convolution fusion | flops 25169920 | bytes 2622464 | tf_op jit(solution)/shard_map/eskp,eslpq->eslkq/dot_general | solution.py:89
  75.3 0.7 fusion.23
  76.0 0.6 fusion.18
  76.6 0.6 fusion.17
  77.2 0.6 fusion.47
  77.7 0.6 fusion.16
  78.3 0.1 collective-permute-start.6
  78.4 7.5 %collective-permute-start.7 = (f32[16,4,16,128]{3,2,1,0:T(8,128)S(1)}, f32[16,4,16,128]{3,2,1,0:T(8,128)S(1)}, u32[]{:S(2)}, u32[]{:S(2)}) collective-permute-start(f32[16,4,16,128]{3,2,1,0:T(8,128)S(1)} %fusion.16), channel_id=1, source_target_pairs={{1,0},{2,1},{3,2},{4,3},{5,4},{6,5},{7,6},{8,7},{9,8},{10,9},{11,1... | collective-permute-start | bytes 1572872 | tf_op jit(solution)/shard_map/ppermute | solution.py:19
  85.9 6.8 %collective-permute-done.6 = f32[16,4,16,128]{3,2,1,0:T(8,128)S(1)} collective-permute-done((f32[16,4,16,128]{3,2,1,0:T(8,128)S(1)}, f32[16,4,16,128]{3,2,1,0:T(8,128)S(1)}, u32[]{:S(2)}, u32[]{:S(2)}) %collective-permute-start.6) | collective-permute-done | bytes 524320 | tf_op jit(solution)/shard_map/ppermute | solution.py:18
  92.7 0.0 collective-permute-done.7
  92.7 0.1 pad_maximum_fusion.3
  92.8 2.0 %gather_fusion.3 = f32[64,4,16,128]{3,2,1,0:T(8,128)} fusion(f32[48,4,16,128]{3,2,1,0:T(8,128)S(1)} %pad_maximum_fusion.3, s32[1024]{0:T(1024)S(1)} %pad_clamp_fusion), kind=kCustom, calls=%fused_computation.3 | custom fusion | bytes 4194560 | tf_op jit(solution)/shard_map/gather | solution.py:121
  94.8 2.4 %convolution_bitcast_fusion = f32[16,4,4,4,128]{4,3,2,1,0:T(4,128)S(1)} fusion(f32[16,4,4,16,128]{4,3,2,1,0:T(8,128)} %bitcast.111, s32[16,4,4]{2,1,0:T(4,128)S(1)} %copy.35), kind=kOutput, calls=%fused_computation.20 | convolution fusion | flops 25169920 | bytes 2622464 | tf_op jit(solution)/shard_map/eskp,eslpq->eslkq/dot_general | solution.py:89
  97.3 1.5 %fusion.27 = f32[16,4,16,128]{3,2,1,0:T(8,128)} fusion(f32[16,4,16,128]{3,2,1,0:T(8,128)S(1)} %add.135, f32[16,4,16,128]{3,2,1,0:T(8,128)S(1)} %fusion.16, f32[16,4,4,4,128]{4,3,2,1,0:T(4,128)S(1)} %convolution_bitcast_fusion, f32[16]{0:T(128)S(1)} %copy-done.5, f32[4,4,16,1,1]{2,1,0,4,3:T(4,128)S(1)} %copy-done.3), kind=kOutput, calls=%fused_computation.41 | convolution fusion | flops 25690112 | bytes 2098240 | tf_op jit(solution)/shard_map/skp,eslkq->elpq/dot_general | solution.py:95
  (13 shorter events, 0.1 us)
Async XLA Ops:
  0.0 15.3 %collective-permute-start = (f32[16,4,16,128]{3,2,1,0:T(8,128)}, f32[16,4,16,128]{3,2,1,0:T(8,128)S(1)}, u32[]{:S(2)}, u32[]{:S(2)}) collective-permute-start(f32[16,4,16,128]{3,2,1,0:T(8,128)} %param.18), channel_id=1, source_target_pairs={{0,1},{1,2},{2,3},{3,4},{4,5},{5,6},{6,7},{7,8},{8,9},{9,10},{10,1... | collective-permute-start | bytes 1572872 | tf_op jit(solution)/shard_map/ppermute | solution.py:18
  0.0 15.3 %collective-permute-start.1 = (f32[16,4,16,128]{3,2,1,0:T(8,128)}, f32[16,4,16,128]{3,2,1,0:T(8,128)S(1)}, u32[]{:S(2)}, u32[]{:S(2)}) collective-permute-start(f32[16,4,16,128]{3,2,1,0:T(8,128)} %param.18), channel_id=1, source_target_pairs={{1,0},{2,1},{3,2},{4,3},{5,4},{6,5},{7,6},{8,7},{9,8},{10,9},{11,1... | collective-permute-start | bytes 1572872 | tf_op jit(solution)/shard_map/ppermute | solution.py:19
  22.8 4.6 %copy-start = (f32[16,4,16,128]{3,2,1,0:T(8,128)S(1)}, f32[16,4,16,128]{3,2,1,0:T(8,128)}, u32[]{:S(2)}) copy-start(f32[16,4,16,128]{3,2,1,0:T(8,128)} %param.19) | copy-start | bytes 1572868
  22.8 12.2 %copy-start.4 = (f32[16,2,16]{2,1,0:T(2,128)S(1)}, f32[16,2,16]{2,1,0:T(2,128)}, u32[]{:S(2)}) copy-start(f32[16,2,16]{2,1,0:T(2,128)} %param.25) | copy-start | bytes 6148
  27.5 14.1 %collective-permute-start.2 = (f32[16,4,16,128]{3,2,1,0:T(8,128)S(1)}, f32[16,4,16,128]{3,2,1,0:T(8,128)S(1)}, u32[]{:S(2)}, u32[]{:S(2)}) collective-permute-start(f32[16,4,16,128]{3,2,1,0:T(8,128)S(1)} %add.134), channel_id=1, source_target_pairs={{0,1},{1,2},{2,3},{3,4},{4,5},{5,6},{6,7},{7,8},{8,9},{9,10},{10,1... | collective-permute-start | bytes 1572872 | tf_op jit(solution)/shard_map/ppermute | solution.py:18
  27.6 14.1 %collective-permute-start.3 = (f32[16,4,16,128]{3,2,1,0:T(8,128)S(1)}, f32[16,4,16,128]{3,2,1,0:T(8,128)S(1)}, u32[]{:S(2)}, u32[]{:S(2)}) collective-permute-start(f32[16,4,16,128]{3,2,1,0:T(8,128)S(1)} %add.134), channel_id=1, source_target_pairs={{1,0},{2,1},{3,2},{4,3},{5,4},{6,5},{7,6},{8,7},{9,8},{10,9},{11,1... | collective-permute-start | bytes 1572872 | tf_op jit(solution)/shard_map/ppermute | solution.py:19
  48.2 4.7 %copy-start.2 = (f32[16,16,1,1]{1,0,3,2:T(8,128)S(1)}, f32[16,16,1,1]{1,0,3,2:T(8,128)}, u32[]{:S(2)}) copy-start(f32[16,16,1,1]{1,0,3,2:T(8,128)} %constant.107) | copy-start | bytes 3076
  52.8 1.3 %copy-start.1 = (f32[16,16,1,1]{1,0,3,2:T(8,128)S(1)}, f32[16,16,1,1]{1,0,3,2:T(8,128)}, u32[]{:S(2)}) copy-start(f32[16,16,1,1]{1,0,3,2:T(8,128)} %constant.108) | copy-start | bytes 3076
  53.4 9.7 %copy-start.6 = (s32[16,4]{0,1:T(4,128)S(1)}, s32[16,4]{0,1:T(4,128)}, u32[]{:S(2)}) copy-start(s32[16,4]{0,1:T(4,128)} %param.24) | copy-start | bytes 772
  53.4 9.7 %copy-start.7 = (s32[4,4]{1,0:T(4,128)S(1)}, s32[4,4]{1,0:T(4,128)}, u32[]{:S(2)}) copy-start(s32[4,4]{1,0:T(4,128)} %constant.94.clone) | copy-start | bytes 196
  55.2 14.3 %collective-permute-start.4 = (f32[16,4,16,128]{3,2,1,0:T(8,128)S(1)}, f32[16,4,16,128]{3,2,1,0:T(8,128)S(1)}, u32[]{:S(2)}, u32[]{:S(2)}) collective-permute-start(f32[16,4,16,128]{3,2,1,0:T(8,128)S(1)} %fusion.19), channel_id=1, source_target_pairs={{0,1},{1,2},{2,3},{3,4},{4,5},{5,6},{6,7},{7,8},{8,9},{9,10},{10,1... | collective-permute-start | bytes 1572872 | tf_op jit(solution)/shard_map/ppermute | solution.py:18
  55.3 14.3 %collective-permute-start.5 = (f32[16,4,16,128]{3,2,1,0:T(8,128)S(1)}, f32[16,4,16,128]{3,2,1,0:T(8,128)}, u32[]{:S(2)}, u32[]{:S(2)}) collective-permute-start(f32[16,4,16,128]{3,2,1,0:T(8,128)S(1)} %fusion.19), channel_id=1, source_target_pairs={{1,0},{2,1},{3,2},{4,3},{5,4},{6,5},{7,6},{8,7},{9,8},{10,9},{11,1... | collective-permute-start | bytes 1572872 | tf_op jit(solution)/shard_map/ppermute | solution.py:19
  72.8 2.5 %copy-start.3 = (f32[4,4,16,1,1]{2,1,0,4,3:T(4,128)S(1)}, f32[4,4,16,1,1]{2,1,0,4,3:T(4,128)}, u32[]{:S(2)}) copy-start(f32[4,4,16,1,1]{2,1,0,4,3:T(4,128)} %constant.110) | copy-start | bytes 3076
  72.8 2.5 %copy-start.5 = (f32[16]{0:T(128)S(1)}, f32[16]{0:T(128)}, u32[]{:S(2)}) copy-start(f32[16]{0:T(128)} %constant.105) | copy-start | bytes 196
  78.3 14.4 %collective-permute-start.6 = (f32[16,4,16,128]{3,2,1,0:T(8,128)S(1)}, f32[16,4,16,128]{3,2,1,0:T(8,128)S(1)}, u32[]{:S(2)}, u32[]{:S(2)}) collective-permute-start(f32[16,4,16,128]{3,2,1,0:T(8,128)S(1)} %fusion.16), channel_id=1, source_target_pairs={{0,1},{1,2},{2,3},{3,4},{4,5},{5,6},{6,7},{7,8},{8,9},{9,10},{10,1... | collective-permute-start | bytes 1572872 | tf_op jit(solution)/shard_map/ppermute | solution.py:18
  78.4 14.3 %collective-permute-start.7 = (f32[16,4,16,128]{3,2,1,0:T(8,128)S(1)}, f32[16,4,16,128]{3,2,1,0:T(8,128)S(1)}, u32[]{:S(2)}, u32[]{:S(2)}) collective-permute-start(f32[16,4,16,128]{3,2,1,0:T(8,128)S(1)} %fusion.16), channel_id=1, source_target_pairs={{1,0},{2,1},{3,2},{4,3},{5,4},{6,5},{7,6},{8,7},{9,8},{10,9},{11,1... | collective-permute-start | bytes 1572872 | tf_op jit(solution)/shard_map/ppermute | solution.py:19
where the time goes:
time: 99.3 us; the launch traced here: 98.8 us
  starting transfers between devices  31 us (31%)
  matrix products  29 us (29%)
  waiting for transfers between devices  23.1 us (23%)
  local copies, waits for them, and re-layouts  10.1 us (10%)
  other arithmetic  5.24 us (5%)
    ppermute x4, starting transfers between devices, extended_2(): after = lax.ppermute(first, axis, down)  30.8 us
    ppermute x4, waiting for transfers between devices, extended_2(): before = lax.ppermute(last, axis, up)  22.8 us
    dot_general x2, matrix products, candidate_mix(): return jnp.einsum('elpc,eclpq->elpq', matched, mixed, precision=HIGH)  9.13 us
    dot_general x2, matrix products, candidate_mix(): mixed = jnp.einsum('elpj,ecljq->eclpq', shaped, candidates, precision=HIGH)  8.22 us
    dot_general x2, matrix products, partner_edges(): return jnp.einsum('eskp,eslpq->eslkq', select, gathered, precision=HIGH)  4.92 us
    gather x2, local copies, waits for them, and re-layouts, candidate_mix(): candidates = table[cand_index]  4.44 us
    gather x2, local copies, waits for them, and re-layouts, edge_close(): extended[offset * local_count + slot_of]  4.04 us
    concatenate x4, other arithmetic, extended_2(): x = jnp.concatenate([before, x, after], axis=dim)  2.59 us
  transfers between devices with their start and end apart: 8, of which 6 were waited for; matrix products, arithmetic and copies ran while one was open for 4% of the time, Pallas kernels for 0%

commit v1 on v0

v1 whole, which is shorter than its diff:
```python
import functools

import jax
import jax.numpy as jnp
import numpy as np
from jax import lax
from jax.experimental import pallas as pl
from jax.experimental.pallas import tpu as pltpu
from jax.sharding import PartitionSpec as P

VISCOSITY = 0.002
HIGH = lax.Precision.HIGHEST
LEV = 4
PTS = 256
Q = 128
F32 = jnp.float32
BF16 = jnp.bfloat16
I32 = jnp.int32


def derivative_matrix():
    nodes = np.array([-1.0, -np.sqrt(0.2), np.sqrt(0.2), 1.0])
    count = nodes.shape[0]
    bary = np.array(
        [1.0 / np.prod([nodes[j] - nodes[m] for m in range(count) if m != j]) for j in range(count)]
    )
    derivative = np.zeros((count, count))
    for i in range(count):
        for j in range(count):
            if i != j:
                derivative[i, j] = bary[j] / bary[i] / (nodes[i] - nodes[j])
        derivative[i, i] = -np.sum(derivative[i])
    return derivative


def rows(shape):
    return lax.broadcasted_iota(I32, shape, 0)


def cols(shape):
    return lax.broadcasted_iota(I32, shape, 1)


def dot(a, b):
    return jnp.dot(a, b, preferred_element_type=F32)


def dot_exact(a, b):
    return jnp.dot(a, b, preferred_element_type=F32, precision=HIGH)


def split(x):
    hi = x.astype(BF16)
    lo = (x - hi.astype(F32)).astype(BF16)
    return hi, lo


def dot3(a_hi, a_lo, b_hi, b_lo):
    return dot(a_hi, b_hi) + (dot(a_hi, b_lo) + dot(a_lo, b_hi))


def edge_point(s, k):
    return jnp.where(s == 0, 4 * k, jnp.where(s == 1, 12 + k, jnp.where(s == 2, 15 - 4 * k, 3 - k)))


def direction_table(shape, along_b):
    m, p = rows(shape) & 15, cols(shape) & 15
    if along_b:
        i, j, live = m & 3, p & 3, (m >> 2) == (p >> 2)
    else:
        i, j, live = m >> 2, p >> 2, (m & 3) == (p & 3)
    which = jnp.where(live, i * 4 + j, -1)
    table = derivative_matrix()
    value = jnp.zeros(shape, F32)
    for at in range(16):
        value = jnp.where(which == at, np.float32(table[at // 4, at % 4]), value)
    return value


def offset_of(owner, me, count):
    d = owner - me
    d = jnp.where(d > 1, d - count, d)
    d = jnp.where(d < -1, d + count, d)
    return d + 1


def kernel(
    count,
    tracers, sources, weights, dep_owner, dep_slot, nbr_elem, nbr_edge, metric,
    out,
    own_t, src, wts, dow, dsl, nel, ned, met,
    f1, first, f2, second, part, outbuf,
    w_hi, w_lo,
    v_out, v_in, s3, x3,
    h_hi, h_lo, sm_hi, sm_lo, e_hi, e_lo,
    loc, loc_t, loc_o,
    send1, recv1, send2, recv2, send3, recv3, sendv, recvv,
):
    me = lax.axis_index("elem")

    def at(step):
        return lax.rem(me + step + count, count)

    small = [
        pltpu.make_async_copy(a, b, loc.at[i])
        for i, (a, b) in enumerate(
            [
                (weights, wts),
                (dep_owner, dow),
                (dep_slot, dsl),
                (nbr_elem, nel),
                (nbr_edge, ned),
                (metric, met),
            ]
        )
    ]
    load_t = [pltpu.make_async_copy(tracers.at[:, k], own_t.at[k], loc_t.at[0, k]) for k in range(LEV)]
    load_s = [pltpu.make_async_copy(sources.at[:, k], src.at[k], loc_t.at[1, k]) for k in range(LEV)]

    def remote(source, target, send_sem, recv_sem, step):
        return pltpu.make_async_remote_copy(
            src_ref=source,
            dst_ref=target,
            send_sem=send_sem,
            recv_sem=recv_sem,
            device_id=(at(step),),
            device_id_type=pl.DeviceIdType.MESH,
        )

    ex1 = [
        [remote(own_t.at[k], f1.at[k, i], send1.at[k, i], recv1.at[k, i], (1, -1)[i]) for i in range(2)]
        for k in range(LEV)
    ]
    ex2 = [
        [remote(first.at[k], f2.at[k, i], send2.at[k, i], recv2.at[k, i], (1, -1)[i]) for i in range(2)]
        for k in range(LEV)
    ]
    exv = [
        remote(v_out.at[pl.ds(64 * i, 64)], v_in.at[i], sendv.at[i], recvv.at[i], (1, -1)[i])
        for i in range(2)
    ]
    spans = [(0, 128, 0, 1), (128, 128, 128, -1), (0, 64, 256, 2), (128, 64, 320, -2)]
    ex3 = [
        [
            remote(
                s3.at[k, pl.ds(a, size)], x3.at[k, pl.ds(b, size)], send3.at[k, i], recv3.at[k, i], step
            )
            for i, (a, size, b, step) in enumerate(spans)
        ]
        for k in range(LEV)
    ]

    barrier = pltpu.get_barrier_semaphore()
    for step in (1, -1, 2, -2):
        pl.semaphore_signal(
            barrier, inc=1, device_id=(at(step),), device_id_type=pl.DeviceIdType.MESH
        )
    for c in load_t:
        c.start()
    for c in small:
        c.start()
    for c in load_s:
        c.start()
    for c in load_t:
        c.wait()
    pl.semaphore_wait(barrier, 4)
    for k in range(LEV):
        for c in ex1[k]:
            c.start()

    for c in small:
        c.wait()
    for c in load_s:
        c.wait()
    diagonal = (cols((16, PTS)) >> 4) == rows((16, PTS))
    eye16 = cols((16, 16)) == rows((16, 16))
    tile_j = ((rows((PTS, PTS)) & 15) == (cols((PTS, PTS)) & 15)).astype(F32).astype(BF16)
    lane_elem = (cols((1, PTS)) >> 4).astype(F32)

    def advection_matrix(k):
        his, los, codes = [], [], []
        for e in range(16):
            row = wts[e, pl.ds(k, 1), :]
            hi = row.astype(BF16).astype(F32)
            his.append(jnp.where(diagonal, jnp.broadcast_to(hi, (16, PTS)), 0.0))
            los.append(jnp.where(diagonal, jnp.broadcast_to(row - hi, (16, PTS)), 0.0))
            code = offset_of(dow[e, pl.ds(k, 1), :], me, count) * 16 + dsl[e, pl.ds(k, 1), :]
            codes.append(jnp.where(eye16, jnp.broadcast_to(code.astype(F32), (16, 16)), 0.0))
        hi = dot(jnp.concatenate(his, axis=0).astype(BF16), tile_j)
        lo = dot(jnp.concatenate(los, axis=0).astype(BF16), tile_j)
        code = jnp.sum(jnp.concatenate(codes, axis=0), axis=1, keepdims=True)
        for i in range(3):
            match = code == (lane_elem + float(16 * i))
            w_hi[k, i] = jnp.where(match, hi, 0.0).astype(BF16)
            w_lo[k, i] = jnp.where(match, lo, 0.0).astype(BF16)

    def mix(k, i, field):
        hi, lo = split(field.reshape(PTS, Q))
        return dot3(w_hi[k, i], w_lo[k, i], hi, lo)

    def cube(x):
        return x.reshape(16, 16, Q)

    for k in range(LEV):
        advection_matrix(k)
        first[k] = cube(mix(k, 1, own_t[k])) + src[k]

    square = (PTS, PTS)
    r, c = rows(square), cols(square)
    same_elem = (r >> 4) == (c >> 4)
    unit = r == c
    left_a, left_b = direction_table((16, 16), False), direction_table((16, 16), True)
    right_a, right_b = direction_table((16, PTS), False), direction_table((16, PTS), True)
    fa, fb, ne_rows, nt_rows = [], [], [], []
    pick = (rows((16, 4)) >> 2) == cols((16, 4))
    for e in range(16):
        fa.append(left_a * jnp.broadcast_to(met[e, pl.ds(0, 1), :], (16, 16)))
        fb.append(left_b * jnp.broadcast_to(met[e, pl.ds(1, 1), :], (16, 16)))
        ne_rows.append(jnp.where(pick, jnp.broadcast_to(nel[pl.ds(e, 1), :], (16, 4)), 0).astype(F32))
        nt_rows.append(jnp.where(pick, jnp.broadcast_to(ned[pl.ds(e, 1), :], (16, 4)), 0).astype(F32))
    full = dot_exact(jnp.concatenate(fa, axis=0), right_a) + dot_exact(jnp.concatenate(fb, axis=0), right_b)
    m = jnp.where(same_elem, full, 0.0)

    ne = jnp.sum(jnp.concatenate(ne_rows, axis=0), axis=1, keepdims=True).astype(I32)
    nt = jnp.sum(jnp.concatenate(nt_rows, axis=0), axis=1, keepdims=True).astype(I32)
    off = offset_of(ne >> 4, me, count)
    pe = (ne & 15) * 4 + nt
    off_f, pe_f = off.astype(F32), pe.astype(F32)
    off_row = jnp.sum(jnp.where(unit, off_f, 0.0), axis=0, keepdims=True)
    pe_row = jnp.sum(jnp.where(unit, pe_f, 0.0), axis=0, keepdims=True)
    peer = (off_row == off_f) & ((c & 3) == 0)
    rank_own = jnp.sum(jnp.where(peer & ((c >> 2) < (r >> 2)), 1.0, 0.0), axis=1, keepdims=True).astype(I32)
    rank_pe = jnp.sum(jnp.where(peer & (pe_row < pe_f), 1.0, 0.0), axis=1, keepdims=True).astype(I32)
    point = rows((PTS, 1)) & 3
    slot = jnp.where(off == 1, pe, jnp.where(off == 0, 64 + rank_pe, 80 + rank_pe))
    take = (cols((PTS, 384)) == slot * 4 + 3 - point).astype(F32).astype(BF16)
    place = jnp.where(off == 1, -1, jnp.where(off == 2, 0, 64) + rank_own * 4 + point)
    pack_t = (cols((PTS, 128)) == place).astype(F32)
    pack = pack_t.T.astype(BF16)
    spread_t = (same_elem & ((r & 15) == edge_point((c >> 2) & 3, c & 3))).astype(F32).astype(BF16)
    spread = (same_elem & ((c & 15) == edge_point((r >> 2) & 3, r & 3))).astype(F32).astype(BF16)
    a, b = (rows((PTS, 1)) >> 2) & 3, rows((PTS, 1)) & 3
    rim_a, rim_b = ((a == 0) | (a == 3)).astype(F32), ((b == 0) | (b == 3)).astype(F32)
    counts = 1.0 + rim_a + rim_b
    added = dot(spread_t, take)
    own_add = dot(added[:, :PTS].astype(BF16), spread)
    r_own = (jnp.where(unit, 1.0, 0.0) + own_add) / counts
    r_out = added[:, PTS:] / counts
    picked = dot(pack, spread)
    km = dot_exact(picked, m)
    g = dot_exact(r_own, m)
    v = dot_exact(km, r_out)
    v_out[...] = v
    for cpy in exv:
        cpy.start()
    kmg = dot_exact(km, g)
    sm = jnp.concatenate([km[:64], kmg[:64], km[64:], kmg[64:]], axis=0)
    hi, lo = split(sm)
    sm_hi[...] = hi
    sm_lo[...] = lo
    gr = dot_exact(g, r_out)
    gg = dot_exact(g, g)

    for k in range(LEV):
        total = first[k].reshape(PTS, Q)
        for i in range(2):
            ex1[k][i].wait_recv()
            total = total + mix(k, 2 * i, f1[k, i])
        first[k] = cube(total)
        for cpy in ex2[k]:
            cpy.start()
        part[k] = mix(k, 1, total) + src[k].reshape(PTS, Q)

    for cpy in exv:
        cpy.wait_recv()
    from_prev, from_next = v_in[0], v_in[1]
    rv_p = dot_exact(r_out[:, :64], from_prev)
    rv_n = dot_exact(r_out[:, 64:], from_next)
    twice = gg + dot_exact(rv_p[:, 64:], km[64:]) + dot_exact(rv_n[:, :64], km[:64])
    h = jnp.where(unit, 1.0, 0.0) - VISCOSITY * twice
    hi, lo = split(h)
    h_hi[...] = hi
    h_lo[...] = lo
    ext = -VISCOSITY * jnp.concatenate(
        [gr[:, :64], r_out[:, :64], gr[:, 64:], r_out[:, 64:], rv_p[:, :64], rv_n[:, 64:]], axis=1
    )
    hi, lo = split(ext)
    e_hi[...] = hi
    e_lo[...] = lo

    for k in range(LEV):
        total = part[k]
        for i in range(2):
            ex2[k][i].wait_recv()
            total = total + mix(k, 2 * i, f2[k, i])
        hi, lo = split(total)
        s3[k] = dot3(sm_hi[...], sm_lo[...], hi, lo)
        for cpy in ex3[k]:
            cpy.start()
        part[k] = dot3(h_hi[...], h_lo[...], hi, lo)

    stores = []
    for k in range(LEV):
        for cpy in ex3[k]:
            cpy.wait_recv()
        hi, lo = split(x3[k])
        outbuf[k] = cube(part[k] + dot3(e_hi[...], e_lo[...], hi, lo))
        store = pltpu.make_async_copy(outbuf.at[k], out.at[:, k], loc_o.at[k])
        store.start()
        stores.append(store)
    for group in ex1 + ex2 + ex3 + [exv]:
        for cpy in group:
            cpy.wait_send()
    for store in stores:
        store.wait()


def local(tracers, sources, weights, dep_owner, dep_slot, nbr_elem, nbr_edge, metric):
    count = lax.axis_size("elem")
    block = (LEV, 16, 16, Q)
    dma = pltpu.SemaphoreType.DMA
    vmem = pltpu.VMEM
    scratch = [
        vmem(block, F32), vmem(block, F32), vmem(weights.shape, F32),
        vmem(dep_owner.shape, I32), vmem(dep_slot.shape, I32),
        vmem(nbr_elem.shape, I32), vmem(nbr_edge.shape, I32), vmem(metric.shape, F32),
        vmem((LEV, 2, 16, 16, Q), F32), vmem(block, F32), vmem((LEV, 2, 16, 16, Q), F32),
        vmem((8, 128), F32), vmem((LEV, PTS, Q), F32), vmem(block, F32),
        vmem((LEV, 3, PTS, PTS), BF16), vmem((LEV, 3, PTS, PTS), BF16),
        vmem((128, 128), F32), vmem((2, 64, 128), F32),
        vmem((LEV, PTS, Q), F32), vmem((LEV, 384, Q), F32),
        vmem((PTS, PTS), BF16), vmem((PTS, PTS), BF16),
        vmem((PTS, PTS), BF16), vmem((PTS, PTS), BF16),
        vmem((PTS, 384), BF16), vmem((PTS, 384), BF16),
        dma((6,)), dma((2, LEV)), dma((LEV,)),
        dma((LEV, 2)), dma((LEV, 2)), dma((LEV, 2)), dma((LEV, 2)),
        dma((LEV, 4)), dma((LEV, 4)), dma((2,)), dma((2,)),
    ]
    return pl.pallas_call(
        functools.partial(kernel, count),
        out_shape=jax.ShapeDtypeStruct(tracers.shape, F32),
        in_specs=[pl.BlockSpec(memory_space=pl.ANY)] * 8,
        out_specs=pl.BlockSpec(memory_space=pl.ANY),
        scratch_shapes=scratch,
        compiler_params=pltpu.CompilerParams(collective_id=0, has_side_effects=True),
        name="tracer_step",
    )(tracers, sources, weights, dep_owner, dep_slot, nbr_elem, nbr_edge, metric)


def solution(mesh):
    placed = (
        P("elem", None, None, None),
        P("elem", None, None, None),
        P("elem", None, None),
        P("elem", None, None),
        P("elem", None, None),
        P("elem", None),
        P("elem", None),
        P("elem", None, None),
    )
    return jax.shard_map(
        local, mesh=mesh, in_specs=placed, out_specs=P("elem", None, None, None), check_vma=False
    )
```

time: 99.3 us -> 39.4 us (0.40)
  the two profiles are of different devices: /device:TPU:0 before, /device:TPU:1 now
where the time goes in v1:
time: 39.4 us; the launch traced here: 39.2 us
  Pallas kernels  35.2 us (89%)
  local copies, waits for them, and re-layouts  3.93 us (10%)
    pallas_call x1, Pallas kernels, local(): pl.pallas_call(functools.partial(kernel, count), out_shape=jax.ShapeDtype...  35.2 us
    unnamed x5, local copies, waits for them, and re-layouts  3.93 us

profile of v1, /device:TPU:1, one launch (start us, length us, event | category | flops | bytes accessed | tf_op | source)
XLA Modules:
  0.0 39.2 jit_solution(13356911729724909800)
XLA Ops:
  0.0 0.0 copy-start
  0.0 1.4 %copy.9.nbr_elem = s32[16,4]{1,0:T(8,128)} copy(s32[16,4]{0,1:T(4,128)} %param.13) | data formatting | bytes 512 | tf_op args[5]
  1.4 0.0 copy-done
  1.4 0.7 %copy.10.nbr_edge = s32[16,4]{1,0:T(8,128)} copy(s32[16,4]{0,1:T(4,128)S(1)} %copy-done) | data formatting | bytes 512 | tf_op args[6]
  2.0 35.2 %tracer_step.1 = f32[16,4,16,128]{3,2,1,0:T(8,128)} custom-call(f32[16,4,16,128]{3,2,1,0:T(8,128)} %tracers.1, f32[16,4,16,128]{3,2,1,0:T(8,128)} %sources.1, f32[16,4,256]{2,1,0:T(4,128)} %weights.1, s32[16,4,16]{2,1,0:T(4,128)} %dep_owner.1, s32[16,4,16]{2,1,0:T(4,128)} %dep_slot.1, s32[16,4]{1,0:T(8,128)} %copy.9.nbr_elem, s32[16,4]{1,0:T(8,128)} %copy.10.nbr_edge, ...), custom_call_target="tpu_custom_call" | custom-call | tf_op jit(solution)/shard_map/tracer_step/pallas_call | solution.py:339
  37.3 1.9 %copy.12 = f32[16,4,16,128]{3,2,1,0:T(8,128)} copy(f32[16,4,16,128]{3,2,1,0:T(8,128)} %tracer_step.1) | data formatting | bytes 1048576
Async XLA Ops:
  0.0 1.4 %copy-start = (s32[16,4]{0,1:T(4,128)S(1)}, s32[16,4]{0,1:T(4,128)}, u32[]{:S(2)}) copy-start(s32[16,4]{0,1:T(4,128)} %param.14) | copy-start | bytes 772

commit v2 on v1

--- a/solution.py
+++ b/solution.py
@@ -87,13 +87,13 @@
 def kernel(
     count,
     tracers, sources, weights, dep_owner, dep_slot, nbr_elem, nbr_edge, metric,
-    out,
+    outbuf,
     own_t, src, wts, dow, dsl, nel, ned, met,
-    f1, first, f2, second, part, outbuf,
+    f1, first, f2, part,
     w_hi, w_lo,
     v_out, v_in, s3, x3,
     h_hi, h_lo, sm_hi, sm_lo, e_hi, e_lo,
-    loc, loc_t, loc_o,
+    loc, loc_t,
     send1, recv1, send2, recv2, send3, recv3, sendv, recvv,
 ):
     me = lax.axis_index("elem")
@@ -211,18 +211,24 @@
     unit = r == c
     left_a, left_b = direction_table((16, 16), False), direction_table((16, 16), True)
     right_a, right_b = direction_table((16, PTS), False), direction_table((16, PTS), True)
-    fa, fb, ne_rows, nt_rows = [], [], [], []
-    pick = (rows((16, 4)) >> 2) == cols((16, 4))
+    fa, fb = [], []
     for e in range(16):
         fa.append(left_a * jnp.broadcast_to(met[e, pl.ds(0, 1), :], (16, 16)))
         fb.append(left_b * jnp.broadcast_to(met[e, pl.ds(1, 1), :], (16, 16)))
-        ne_rows.append(jnp.where(pick, jnp.broadcast_to(nel[pl.ds(e, 1), :], (16, 4)), 0).astype(F32))
-        nt_rows.append(jnp.where(pick, jnp.broadcast_to(ned[pl.ds(e, 1), :], (16, 4)), 0).astype(F32))
     full = dot_exact(jnp.concatenate(fa, axis=0), right_a) + dot_exact(jnp.concatenate(fb, axis=0), right_b)
     m = jnp.where(same_elem, full, 0.0)
 
-    ne = jnp.sum(jnp.concatenate(ne_rows, axis=0), axis=1, keepdims=True).astype(I32)
-    nt = jnp.sum(jnp.concatenate(nt_rows, axis=0), axis=1, keepdims=True).astype(I32)
+    edge_row, edge_col = rows((PTS, 16)), cols((PTS, 16))
+
+    def edge_column(table):
+        spread_out = jnp.zeros((PTS, 16), F32)
+        for s in range(4):
+            here = ((edge_row >> 4) == edge_col) & (((edge_row >> 2) & 3) == s)
+            line = table[pl.ds(s, 1), :].astype(F32)
+            spread_out = jnp.where(here, jnp.broadcast_to(line, (PTS, 16)), spread_out)
+        return jnp.sum(spread_out, axis=1, keepdims=True).astype(I32)
+
+    ne, nt = edge_column(nel), edge_column(ned)
     off = offset_of(ne >> 4, me, count)
     pe = (ne & 15) * 4 + nt
     off_f, pe_f = off.astype(F32), pe.astype(F32)
@@ -299,20 +305,14 @@
             cpy.start()
         part[k] = dot3(h_hi[...], h_lo[...], hi, lo)
 
-    stores = []
     for k in range(LEV):
         for cpy in ex3[k]:
             cpy.wait_recv()
         hi, lo = split(x3[k])
-        outbuf[k] = cube(part[k] + dot3(e_hi[...], e_lo[...], hi, lo))
-        store = pltpu.make_async_copy(outbuf.at[k], out.at[:, k], loc_o.at[k])
-        store.start()
-        stores.append(store)
+        outbuf[:, k] = cube(part[k] + dot3(e_hi[...], e_lo[...], hi, lo))
     for group in ex1 + ex2 + ex3 + [exv]:
         for cpy in group:
             cpy.wait_send()
-    for store in stores:
-        store.wait()
 
 
 def local(tracers, sources, weights, dep_owner, dep_slot, nbr_elem, nbr_edge, metric):
@@ -323,28 +323,28 @@
     scratch = [
         vmem(block, F32), vmem(block, F32), vmem(weights.shape, F32),
         vmem(dep_owner.shape, I32), vmem(dep_slot.shape, I32),
-        vmem(nbr_elem.shape, I32), vmem(nbr_edge.shape, I32), vmem(metric.shape, F32),
+        vmem(nbr_elem.shape[::-1], I32), vmem(nbr_edge.shape[::-1], I32), vmem(metric.shape, F32),
         vmem((LEV, 2, 16, 16, Q), F32), vmem(block, F32), vmem((LEV, 2, 16, 16, Q), F32),
-        vmem((8, 128), F32), vmem((LEV, PTS, Q), F32), vmem(block, F32),
+        vmem((LEV, PTS, Q), F32),
         vmem((LEV, 3, PTS, PTS), BF16), vmem((LEV, 3, PTS, PTS), BF16),
         vmem((128, 128), F32), vmem((2, 64, 128), F32),
         vmem((LEV, PTS, Q), F32), vmem((LEV, 384, Q), F32),
         vmem((PTS, PTS), BF16), vmem((PTS, PTS), BF16),
         vmem((PTS, PTS), BF16), vmem((PTS, PTS), BF16),
         vmem((PTS, 384), BF16), vmem((PTS, 384), BF16),
-        dma((6,)), dma((2, LEV)), dma((LEV,)),
+        dma((6,)), dma((2, LEV)),
         dma((LEV, 2)), dma((LEV, 2)), dma((LEV, 2)), dma((LEV, 2)),
         dma((LEV, 4)), dma((LEV, 4)), dma((2,)), dma((2,)),
     ]
     return pl.pallas_call(
         functools.partial(kernel, count),
-        out_shape=jax.ShapeDtypeStruct(tracers.shape, F32),
+        out_shape=pltpu.VMEM(tracers.shape, F32),
         in_specs=[pl.BlockSpec(memory_space=pl.ANY)] * 8,
-        out_specs=pl.BlockSpec(memory_space=pl.ANY),
+        out_specs=pl.BlockSpec(memory_space=pltpu.VMEM),
         scratch_shapes=scratch,
         compiler_params=pltpu.CompilerParams(collective_id=0, has_side_effects=True),
         name="tracer_step",
-    )(tracers, sources, weights, dep_owner, dep_slot, nbr_elem, nbr_edge, metric)
+    )(tracers, sources, weights, dep_owner, dep_slot, nbr_elem.T, nbr_edge.T, metric)
 
 
 def solution(mesh):

time: 39.4 us -> 35.5 us (0.901)
  local copies, waits for them, and re-layouts: 3.93 us -> 0.8 us
  Pallas kernels: 35.2 us -> 34.6 us
    unnamed x5 -> x1, local copies, waits for them, and re-layouts: 3.93 us -> 0.8 us
    pallas_call x1, Pallas kernels: 35.2 us -> 34.6 us  [local(): pl.pallas_call(functools.partial(kernel, count), out_shape=pltpu.VMEM(tra...]
where the time goes in v2:
time: 35.5 us; the launch traced here: 35.4 us
  Pallas kernels  34.6 us (97%)
  local copies, waits for them, and re-layouts  0.8 us (2%)
    pallas_call x1, Pallas kernels, local(): pl.pallas_call(functools.partial(kernel, count), out_shape=pltpu.VMEM(tra...  34.6 us
    unnamed x1, local copies, waits for them, and re-layouts  0.8 us

profile of v2, /device:TPU:1, one launch (start us, length us, event | category | flops | bytes accessed | tf_op | source)
XLA Modules:
  0.0 35.4 jit_solution(7923505695090989553)
XLA Ops:
  0.0 34.6 %tracer_step.1 = f32[16,4,16,128]{3,2,1,0:T(8,128)S(1)} custom-call(f32[16,4,16,128]{3,2,1,0:T(8,128)} %tracers.1, f32[16,4,16,128]{3,2,1,0:T(8,128)} %sources.1, f32[16,4,256]{2,1,0:T(4,128)} %weights.1, s32[16,4,16]{2,1,0:T(4,128)} %dep_owner.1, s32[16,4,16]{2,1,0:T(4,128)} %dep_slot.1, s32[4,16]{1,0:T(4,128)} %bitcast.2, s32[4,16]{1,0:T(4,128)} %bitcast.3, ...), custom_call_target="tpu_custom_call" | custom-call | tf_op jit(solution)/shard_map/tracer_step/pallas_call | solution.py:339
  34.6 0.8 %copy.10 = f32[16,4,16,128]{3,2,1,0:T(8,128)} copy(f32[16,4,16,128]{3,2,1,0:T(8,128)S(1)} %tracer_step.1) | data formatting | bytes 1048576

commit v3 on v2

v3 whole, which is shorter than its diff:
```python
import functools

import jax
import jax.numpy as jnp
import numpy as np
from jax import lax
from jax.experimental import pallas as pl
from jax.experimental.pallas import tpu as pltpu
from jax.sharding import PartitionSpec as P

VISCOSITY = 0.002
LEV = 4
PTS = 256
Q = 128
F32 = jnp.float32
BF16 = jnp.bfloat16
I32 = jnp.int32


def derivative_matrix():
    nodes = np.array([-1.0, -np.sqrt(0.2), np.sqrt(0.2), 1.0])
    count = nodes.shape[0]
    bary = np.array(
        [1.0 / np.prod([nodes[j] - nodes[m] for m in range(count) if m != j]) for j in range(count)]
    )
    derivative = np.zeros((count, count))
    for i in range(count):
        for j in range(count):
            if i != j:
                derivative[i, j] = bary[j] / bary[i] / (nodes[i] - nodes[j])
        derivative[i, i] = -np.sum(derivative[i])
    return derivative


def rows(shape):
    return lax.broadcasted_iota(I32, shape, 0)


def cols(shape):
    return lax.broadcasted_iota(I32, shape, 1)


def dot(a, b):
    return jnp.dot(a, b, preferred_element_type=F32)


def split(x):
    hi = x.astype(BF16)
    lo = (x - hi.astype(F32)).astype(BF16)
    return hi, lo


def dot3(a_hi, a_lo, b_hi, b_lo):
    n = b_hi.shape[1]
    both = dot(a_hi, jnp.concatenate([b_hi, b_lo], axis=1))
    return both[:, :n] + (both[:, n:] + dot(a_lo, b_hi))


def dot_split(a, b):
    return dot3(*split(a), *split(b))


def edge_point(s, k):
    return jnp.where(s == 0, 4 * k, jnp.where(s == 1, 12 + k, jnp.where(s == 2, 15 - 4 * k, 3 - k)))


def direction_table(shape, along_b):
    m, p = rows(shape) & 15, cols(shape) & 15
    if along_b:
        i, j, live = m & 3, p & 3, (m >> 2) == (p >> 2)
    else:
        i, j, live = m >> 2, p >> 2, (m & 3) == (p & 3)
    which = jnp.where(live, i * 4 + j, -1)
    table = derivative_matrix()
    value = jnp.zeros(shape, F32)
    for at in range(16):
        value = jnp.where(which == at, np.float32(table[at // 4, at % 4]), value)
    return value


def offset_of(owner, me, count):
    d = owner - me
    d = jnp.where(d > 1, d - count, d)
    d = jnp.where(d < -1, d + count, d)
    return d + 1


def kernel(
    count,
    tracers, sources, weights, dep_owner, dep_slot, nbr_elem, nbr_edge, metric,
    outbuf,
    own_t, src, wx, dow, dsl, nel, ned, met,
    f1, first, f2, base, total,
    w_hi, w_lo, wx_in, nb_hi, nb_lo,
    v_out, v_in, sm, sm_hi, sm_lo, sm_in, sn_hi, sn_lo,
    corr, vz_hi, vz_lo, once, twice_own, twice, once_in, twice_in, terms_in,
    h_hi, h_lo, e_hi, e_lo,
    loc, loc_t,
    send1, recv1, send2, recv2, sendm, recvm, sendp, recvp, sendq, recvq,
):
    me = lax.axis_index("elem")
    place_in_row = lax.rem(me, 8)
    near = jnp.where(place_in_row < 4, 1, 0)
    far = 1 - near
    edge = (place_in_row == 0) | (place_in_row == 7)
    middle = (place_in_row == 3) | (place_in_row == 4)

    def beyond(side):
        return lax.rem(me + 1 - 2 * side + count, count)

    def remote(source, target, send_sem, recv_sem, side):
        return pltpu.make_async_remote_copy(
            src_ref=source,
            dst_ref=target,
            send_sem=send_sem,
            recv_sem=recv_sem,
            device_id=(beyond(side),),
            device_id_type=pl.DeviceIdType.MESH,
        )

    small = [
        pltpu.make_async_copy(a, b, loc.at[i])
        for i, (a, b) in enumerate(
            [
                (weights, wx.at[:, :, pl.ds(0, PTS)]),
                (dep_owner, dow),
                (dep_slot, dsl),
                (nbr_elem, nel),
                (nbr_edge, ned),
                (metric, met),
            ]
        )
    ]
    load_t = [pltpu.make_async_copy(tracers.at[:, k], own_t.at[k], loc_t.at[0, k]) for k in range(LEV)]
    load_s = [pltpu.make_async_copy(sources.at[:, k], src.at[k], loc_t.at[1, k]) for k in range(LEV)]

    def ex1(k, side):
        return remote(own_t.at[k], f1.at[k, side], send1.at[k, side], recv1.at[k, side], side)

    def ex2(k, side):
        return remote(first.at[k], f2.at[k, side], send2.at[k, side], recv2.at[k, side], side)

    def ex_w(side):
        return remote(wx, wx_in.at[side], sendm.at[0, side], recvm.at[0, side], side)

    def ex_v(side):
        return remote(v_out.at[side], v_in.at[side], sendm.at[1, side], recvm.at[1, side], side)

    def ex_s(side):
        return remote(sm.at[side], sm_in.at[side], sendm.at[2, side], recvm.at[2, side], side)

    def ex_p(k, side):
        return remote(once.at[k, side], once_in.at[k, side], sendp.at[k, side], recvp.at[k, side], side)

    def ex_q(k, side):
        return remote(twice.at[k, side], twice_in.at[k, side], sendq.at[k, side], recvq.at[k, side], side)

    barrier = pltpu.get_barrier_semaphore()
    for side in range(2):
        pl.semaphore_signal(
            barrier, inc=1, device_id=(beyond(side),), device_id_type=pl.DeviceIdType.MESH
        )
    for c in load_t:
        c.start()
    for c in small:
        c.start()
    for c in load_s:
        c.start()
    for c in load_t:
        c.wait()
    pl.semaphore_wait(barrier, 2)
    for k in range(LEV):
        for side in range(2):
            ex1(k, side).start()

    for c in small:
        c.wait()
    wx[:, :, pl.ds(PTS, 128)] = jnp.zeros((16, LEV, 128), F32)
    for e in range(16):
        code = offset_of(dow[e], me, count) * 16 + dsl[e]
        wx[e, :, pl.ds(PTS, 16)] = code.astype(F32)
    for c in load_s:
        c.wait()
    diagonal = (cols((16, PTS)) >> 4) == rows((16, PTS))
    eye16 = cols((16, 16)) == rows((16, 16))
    tile_j = ((rows((PTS, PTS)) & 15) == (cols((PTS, PTS)) & 15)).astype(F32).astype(BF16)
    lane_elem = (cols((1, PTS)) >> 4).astype(F32)

    def tiled(table, k):
        his, los, codes = [], [], []
        for e in range(16):
            row = table[e, pl.ds(k, 1), pl.ds(0, PTS)]
            hi = row.astype(BF16).astype(F32)
            his.append(jnp.where(diagonal, jnp.broadcast_to(hi, (16, PTS)), 0.0))
            los.append(jnp.where(diagonal, jnp.broadcast_to(row - hi, (16, PTS)), 0.0))
            code = table[e, pl.ds(k, 1), pl.ds(PTS, 16)]
            codes.append(jnp.where(eye16, jnp.broadcast_to(code, (16, 16)), 0.0))
        hi = dot(jnp.concatenate(his, axis=0).astype(BF16), tile_j)
        lo = dot(jnp.concatenate(los, axis=0).astype(BF16), tile_j)
        code = jnp.sum(jnp.concatenate(codes, axis=0), axis=1, keepdims=True)
        return hi, lo, code

    def mix(k, i, field):
        hi, lo = split(field.reshape(PTS, Q))
        return dot3(w_hi[k, i], w_lo[k, i], hi, lo)

    def cube(x):
        return x.reshape(16, 16, Q)

    for k in range(LEV):
        hi, lo, code = tiled(wx, k)
        for i in range(3):
            match = code == (lane_elem + float(16 * i))
            w_hi[k, i] = jnp.where(match, hi, 0.0).astype(BF16)
            w_lo[k, i] = jnp.where(match, lo, 0.0).astype(BF16)
        first[k] = cube(mix(k, 1, own_t[k])) + src[k]

    square = (PTS, PTS)
    r, c = rows(square), cols(square)
    same_elem = (r >> 4) == (c >> 4)
    unit = r == c
    left_a, left_b = direction_table((16, 16), False), direction_table((16, 16), True)
    right_a, right_b = direction_table((16, PTS), False), direction_table((16, PTS), True)
    fa, fb = [], []
    for e in range(16):
        fa.append(left_a * jnp.broadcast_to(met[e, pl.ds(0, 1), :], (16, 16)))
        fb.append(left_b * jnp.broadcast_to(met[e, pl.ds(1, 1), :], (16, 16)))
    full = dot_split(jnp.concatenate(fa, axis=0), right_a) + dot_split(jnp.concatenate(fb, axis=0), right_b)
    m = jnp.where(same_elem, full, 0.0)

    edge_row, edge_col = rows((PTS, 16)), cols((PTS, 16))

    def edge_column(table):
        spread_out = jnp.zeros((PTS, 16), F32)
        for s in range(4):
            here = ((edge_row >> 4) == edge_col) & (((edge_row >> 2) & 3) == s)
            line = table[pl.ds(s, 1), :].astype(F32)
            spread_out = jnp.where(here, jnp.broadcast_to(line, (PTS, 16)), spread_out)
        return jnp.sum(spread_out, axis=1, keepdims=True).astype(I32)

    ne, nt = edge_column(nel), edge_column(ned)
    off = offset_of(ne >> 4, me, count)
    pe = (ne & 15) * 4 + nt
    off_f, pe_f = off.astype(F32), pe.astype(F32)
    off_row = jnp.sum(jnp.where(unit, off_f, 0.0), axis=0, keepdims=True)
    pe_row = jnp.sum(jnp.where(unit, pe_f, 0.0), axis=0, keepdims=True)
    peer = (off_row == off_f) & ((c & 3) == 0)
    rank_own = jnp.sum(jnp.where(peer & ((c >> 2) < (r >> 2)), 1.0, 0.0), axis=1, keepdims=True).astype(I32)
    rank_pe = jnp.sum(jnp.where(peer & (pe_row < pe_f), 1.0, 0.0), axis=1, keepdims=True).astype(I32)
    point = rows((PTS, 1)) & 3
    slot = jnp.where(off == 1, pe, jnp.where(off == 0, 64 + rank_pe, 80 + rank_pe))
    take = (cols((PTS, 384)) == slot * 4 + 3 - point).astype(F32).astype(BF16)
    place = jnp.where(off == 1, -1, jnp.where(off == 2, 0, 64) + rank_own * 4 + point)
    pack_t = (cols((PTS, 128)) == place).astype(F32)
    pack = pack_t.T.astype(BF16)
    spread_t = (same_elem & ((r & 15) == edge_point((c >> 2) & 3, c & 3))).astype(F32).astype(BF16)
    spread = (same_elem & ((c & 15) == edge_point((r >> 2) & 3, r & 3))).astype(F32).astype(BF16)
    a, b = (rows((PTS, 1)) >> 2) & 3, rows((PTS, 1)) & 3
    rim_a, rim_b = ((a == 0) | (a == 3)).astype(F32), ((b == 0) | (b == 3)).astype(F32)
    counts = 1.0 + rim_a + rim_b
    added = dot(spread_t, take)
    own_add = dot(added[:, :PTS].astype(BF16), spread)
    r_own = (jnp.where(unit, 1.0, 0.0) + own_add) / counts
    r_out = added[:, PTS:] / counts
    picked = dot(pack, spread)
    km = dot_split(picked, m)
    g = dot_split(r_own, m)
    v = dot_split(km, r_out)
    v_out[0] = v[:64]
    v_out[1] = v[64:]
    for side, through in enumerate((v[:64, :64], v[64:, 64:])):
        hi, lo = split(through)
        vz_hi[side] = hi
        vz_lo[side] = lo
    kmg = dot_split(km, g)
    sm[0] = jnp.concatenate([km[:64], kmg[:64]], axis=0)
    sm[1] = jnp.concatenate([km[64:], kmg[64:]], axis=0)

    def hand_matrices():
        for side in range(2):
            ex_w(side).start()
            ex_v(side).start()
            ex_s(side).start()

    pl.when(edge)(hand_matrices)
    for side in range(2):
        hi, lo = split(sm[side])
        sm_hi[side] = hi
        sm_lo[side] = lo
    gr = dot_split(g, r_out)
    gg = dot_split(g, g)
    ext = -VISCOSITY * jnp.concatenate([gr[:, :64], r_out[:, :64], gr[:, 64:], r_out[:, 64:]], axis=1)
    hi, lo = split(ext)
    e_hi[...] = hi
    e_lo[...] = lo

    def neighbour_matrices(side):
        ex_w(side).wait_recv()
        shift = jnp.where(side == 0, 32.0, 0.0)
        for k in range(LEV):
            hi, lo, code = tiled(wx_in.at[side], k)
            match = code == (lane_elem + shift)
            nb_hi[k, side] = jnp.where(match, hi, 0.0).astype(BF16)
            nb_lo[k, side] = jnp.where(match, lo, 0.0).astype(BF16)

    def corrections(side):
        ex_s(side).wait_recv()
        hi, lo = split(sm_in[side])
        sn_hi[side] = hi
        sn_lo[side] = lo
        for k in range(LEV):
            hi, lo = split(first[k].reshape(PTS, Q))
            taken = dot3(nb_hi[k, side], nb_lo[k, side], hi, lo)
            hi, lo = split(taken)
            corr[k, side] = dot3(sn_hi[side], sn_lo[side], hi, lo)

    def second_from(k, side, last):
        ex2(k, side).wait_recv()
        part = mix(k, 2 * side, f2[k, side])
        here = base[k]
        hi, lo = split(here + part)
        terms = dot3(sm_hi[side], sm_lo[side], hi, lo)
        once[k, side] = terms[:64]
        twice_own[k, side] = terms[64:]
        ex_p(k, side).start()
        if last:
            hi, lo = split(total[k] + part)
            total[k] = dot3(h_hi[...], h_lo[...], hi, lo)
        else:
            total[k] = here + part

    def relay(k, side):
        ex_p(k, side).wait_recv()
        whole = once_in[k, side] + corr[k, side, pl.ds(0, 64)]
        terms_in[k, side, pl.ds(0, 64)] = whole
        hi, lo = split(whole)
        twice[k, side] = twice_own[k, side] + dot3(vz_hi[side], vz_lo[side], hi, lo)
        ex_q(k, side).start()

    for k in range(LEV):
        value = first[k].reshape(PTS, Q)
        for side in range(2):
            ex1(k, side).wait_recv()
            value = value + mix(k, 2 * side, f1[k, side])
        first[k] = cube(value)
        for side in range(2):
            ex2(k, side).start()
        base[k] = mix(k, 1, value) + src[k].reshape(PTS, Q)

        @pl.when(edge)
        def _():
            if k >= 1:
                second_from(k - 1, near, False)
            if k == 2:
                neighbour_matrices(near)

    @pl.when(edge)
    def _():
        second_from(LEV - 1, near, False)

    @pl.when(jnp.logical_not(edge))
    def _():
        hand_matrices()
        for k in range(LEV):
            second_from(k, near, False)
        neighbour_matrices(near)

    corrections(near)

    @pl.when(jnp.logical_not(middle))
    def _():
        for k in range(LEV):
            relay(k, near)

    neighbour_matrices(far)
    corrections(far)
    for side in range(2):
        ex_v(side).wait_recv()
    from_prev, from_next = v_in[0], v_in[1]
    none = jnp.zeros((64, 64), F32)
    blocks = jnp.concatenate(
        [
            jnp.concatenate([none, from_prev[:, 64:]], axis=1),
            jnp.concatenate([from_next[:, :64], none], axis=1),
        ],
        axis=0,
    )
    h = jnp.where(unit, 1.0, 0.0) - VISCOSITY * (gg + dot_split(dot_split(r_out, blocks), km))
    hi, lo = split(h)
    h_hi[...] = hi
    h_lo[...] = lo

    def finish(k):
        for side in range(2):
            ex_q(k, side).wait_recv()
            terms_in[k, side, pl.ds(64, 64)] = twice_in[k, side] + corr[k, side, pl.ds(64, 64)]
        hi, lo = split(terms_in[k].reshape(PTS, Q))
        outbuf[:, k] = cube(total[k] + dot3(e_hi[...], e_lo[...], hi, lo))

    for j in range(LEV + 1):
        if j < LEV:
            second_from(j, far, True)
        if j >= 1:
            relay(j - 1, far)

            @pl.when(middle)
            def _():
                relay(j - 1, near)

    for k in range(LEV):
        finish(k)
    for side in range(2):
        ex_w(side).wait_send()
        ex_v(side).wait_send()
        ex_s(side).wait_send()
        for k in range(LEV):
            for send in (ex1, ex2, ex_p, ex_q):
                send(k, side).wait_send()


def local(tracers, sources, weights, dep_owner, dep_slot, nbr_elem, nbr_edge, metric):
    count = lax.axis_size("elem")
    block = (LEV, 16, 16, Q)
    dma = pltpu.SemaphoreType.DMA
    vmem = pltpu.VMEM
    pairs = (LEV, 2, 16, 16, Q)
    flat = (LEV, PTS, Q)
    tall = (2, 128, PTS)
    slim = (LEV, 2, 64, Q)
    scratch = [
        vmem(block, F32), vmem(block, F32), vmem((16, LEV, 384), F32),
        vmem(dep_owner.shape, I32), vmem(dep_slot.shape, I32),
        vmem(nbr_elem.shape[::-1], I32), vmem(nbr_edge.shape[::-1], I32), vmem(metric.shape, F32),
        vmem(pairs, F32), vmem(block, F32), vmem(pairs, F32), vmem(flat, F32), vmem(flat, F32),
        vmem((LEV, 3, PTS, PTS), BF16), vmem((LEV, 3, PTS, PTS), BF16),
        vmem((2, 16, LEV, 384), F32), vmem((LEV, 2, PTS, PTS), BF16), vmem((LEV, 2, PTS, PTS), BF16),
        vmem((2, 64, 128), F32), vmem((2, 64, 128), F32),
        vmem(tall, F32), vmem(tall, BF16), vmem(tall, BF16),
        vmem(tall, F32), vmem(tall, BF16), vmem(tall, BF16),
        vmem((LEV, 2, 128, Q), F32), vmem((2, 64, 64), BF16), vmem((2, 64, 64), BF16),
        vmem(slim, F32), vmem(slim, F32), vmem(slim, F32), vmem(slim, F32), vmem(slim, F32),
        vmem((LEV, 2, 128, Q), F32),
        vmem((PTS, PTS), BF16), vmem((PTS, PTS), BF16),
        vmem((PTS, PTS), BF16), vmem((PTS, PTS), BF16),
        dma((6,)), dma((2, LEV)),
        dma((LEV, 2)), dma((LEV, 2)), dma((LEV, 2)), dma((LEV, 2)), dma((3, 2)), dma((3, 2)),
        dma((LEV, 2)), dma((LEV, 2)), dma((LEV, 2)), dma((LEV, 2)),
    ]
    return pl.pallas_call(
        functools.partial(kernel, count),
        out_shape=pltpu.VMEM(tracers.shape, F32),
        in_specs=[pl.BlockSpec(memory_space=pl.ANY)] * 8,
        out_specs=pl.BlockSpec(memory_space=pltpu.VMEM),
        scratch_shapes=scratch,
        compiler_params=pltpu.CompilerParams(collective_id=0, has_side_effects=True),
        name="tracer_step",
    )(tracers, sources, weights, dep_owner, dep_slot, nbr_elem.T, nbr_edge.T, metric)


def solution(mesh):
    placed = (
        P("elem", None, None, None),
        P("elem", None, None, None),
        P("elem", None, None),
        P("elem", None, None),
        P("elem", None, None),
        P("elem", None),
        P("elem", None),
        P("elem", None, None),
    )
    return jax.shard_map(
        local, mesh=mesh, in_specs=placed, out_specs=P("elem", None, None, None), check_vma=False
    )
```

time: 35.5 us -> 32.2 us (0.907)
  the two profiles are of different devices: /device:TPU:1 before, /device:TPU:67 now
where the time goes in v3:
time: 32.2 us; the launch traced here: 32.1 us
  Pallas kernels  31.3 us (97%)
  local copies, waits for them, and re-layouts  0.8 us (2%)
    pallas_call x1, Pallas kernels, local(): pl.pallas_call(functools.partial(kernel, count), out_shape=pltpu.VMEM(tra...  31.3 us
    unnamed x1, local copies, waits for them, and re-layouts  0.8 us

profile of v3, /device:TPU:67, one launch (start us, length us, event | category | flops | bytes accessed | tf_op | source)
XLA Modules:
  0.0 32.1 jit_solution(1354548106788092872)
XLA Ops:
  0.0 31.3 %tracer_step.1 = f32[16,4,16,128]{3,2,1,0:T(8,128)S(1)} custom-call(f32[16,4,16,128]{3,2,1,0:T(8,128)} %tracers.1, f32[16,4,16,128]{3,2,1,0:T(8,128)} %sources.1, f32[16,4,256]{2,1,0:T(4,128)} %weights.1, s32[16,4,16]{2,1,0:T(4,128)} %dep_owner.1, s32[16,4,16]{2,1,0:T(4,128)} %dep_slot.1, s32[4,16]{1,0:T(4,128)} %bitcast.2, s32[4,16]{1,0:T(4,128)} %bitcast.3, ...), custom_call_target="tpu_custom_call" | custom-call | tf_op jit(solution)/shard_map/tracer_step/pallas_call | solution.py:449
  31.3 0.8 %copy.10 = f32[16,4,16,128]{3,2,1,0:T(8,128)} copy(f32[16,4,16,128]{3,2,1,0:T(8,128)S(1)} %tracer_step.1) | data formatting | bytes 1048576

commit v4 on v3

--- a/solution.py
+++ b/solution.py
@@ -96,7 +96,7 @@
     corr, vz_hi, vz_lo, once, twice_own, twice, once_in, twice_in, terms_in,
     h_hi, h_lo, e_hi, e_lo,
     loc, loc_t,
-    send1, recv1, send2, recv2, sendm, recvm, sendp, recvp, sendq, recvq,
+    sent, recv1, recv2, recvm, recvp, recvq,
 ):
     me = lax.axis_index("elem")
     place_in_row = lax.rem(me, 8)
@@ -104,6 +104,7 @@
     far = 1 - near
     edge = (place_in_row == 0) | (place_in_row == 7)
     middle = (place_in_row == 3) | (place_in_row == 4)
+    ahead = jnp.where(middle, far, near)
 
     def beyond(side):
         return lax.rem(me + 1 - 2 * side + count, count)
@@ -131,29 +132,32 @@
             ]
         )
     ]
-    load_t = [pltpu.make_async_copy(tracers.at[:, k], own_t.at[k], loc_t.at[0, k]) for k in range(LEV)]
-    load_s = [pltpu.make_async_copy(sources.at[:, k], src.at[k], loc_t.at[1, k]) for k in range(LEV)]
+    load_t = [pltpu.make_async_copy(tracers.at[:, k], own_t.at[k], loc_t.at[0]) for k in range(LEV)]
+    load_s = [pltpu.make_async_copy(sources.at[:, k], src.at[k], loc_t.at[1]) for k in range(LEV)]
+
+    def wait_bytes(like, semaphore):
+        pltpu.make_async_copy(like, like, semaphore).wait()
 
     def ex1(k, side):
-        return remote(own_t.at[k], f1.at[k, side], send1.at[k, side], recv1.at[k, side], side)
+        return remote(own_t.at[k], f1.at[k, side], sent.at[side], recv1.at[k, side], side)
 
     def ex2(k, side):
-        return remote(first.at[k], f2.at[k, side], send2.at[k, side], recv2.at[k, side], side)
+        return remote(first.at[k], f2.at[k, side], sent.at[side], recv2.at[k, side], side)
 
     def ex_w(side):
-        return remote(wx, wx_in.at[side], sendm.at[0, side], recvm.at[0, side], side)
+        return remote(wx, wx_in.at[side], sent.at[side], recvm.at[side], side)
 
     def ex_v(side):
-        return remote(v_out.at[side], v_in.at[side], sendm.at[1, side], recvm.at[1, side], side)
+        return remote(v_out.at[side], v_in.at[side], sent.at[side], recvm.at[side], side)
 
     def ex_s(side):
-        return remote(sm.at[side], sm_in.at[side], sendm.at[2, side], recvm.at[2, side], side)
+        return remote(sm.at[side], sm_in.at[side], sent.at[side], recvm.at[side], side)
 
     def ex_p(k, side):
-        return remote(once.at[k, side], once_in.at[k, side], sendp.at[k, side], recvp.at[k, side], side)
+        return remote(once.at[k, side], once_in.at[k, side], sent.at[side], recvp.at[k, side], side)
 
     def ex_q(k, side):
-        return remote(twice.at[k, side], twice_in.at[k, side], sendq.at[k, side], recvq.at[k, side], side)
+        return remote(twice.at[k, side], twice_in.at[k, side], sent.at[side], recvq.at[k], side)
 
     barrier = pltpu.get_barrier_semaphore()
     for side in range(2):
@@ -166,8 +170,7 @@
         c.start()
     for c in load_s:
         c.start()
-    for c in load_t:
-        c.wait()
+    wait_bytes(own_t, loc_t.at[0])
     pl.semaphore_wait(barrier, 2)
     for k in range(LEV):
         for side in range(2):
@@ -179,8 +182,7 @@
     for e in range(16):
         code = offset_of(dow[e], me, count) * 16 + dsl[e]
         wx[e, :, pl.ds(PTS, 16)] = code.astype(F32)
-    for c in load_s:
-        c.wait()
+    wait_bytes(src, loc_t.at[1])
     diagonal = (cols((16, PTS)) >> 4) == rows((16, PTS))
     eye16 = cols((16, 16)) == rows((16, 16))
     tile_j = ((rows((PTS, PTS)) & 15) == (cols((PTS, PTS)) & 15)).astype(F32).astype(BF16)
@@ -279,8 +281,8 @@
     def hand_matrices():
         for side in range(2):
             ex_w(side).start()
+            ex_s(side).start()
             ex_v(side).start()
-            ex_s(side).start()
 
     pl.when(edge)(hand_matrices)
     for side in range(2):
@@ -294,27 +296,25 @@
     e_hi[...] = hi
     e_lo[...] = lo
 
-    def neighbour_matrices(side):
-        ex_w(side).wait_recv()
+    def meet(side):
+        wait_bytes(first.at[pl.ds(0, 2)], recvm.at[side])
         shift = jnp.where(side == 0, 32.0, 0.0)
         for k in range(LEV):
             hi, lo, code = tiled(wx_in.at[side], k)
             match = code == (lane_elem + shift)
             nb_hi[k, side] = jnp.where(match, hi, 0.0).astype(BF16)
             nb_lo[k, side] = jnp.where(match, lo, 0.0).astype(BF16)
-
-    def corrections(side):
-        ex_s(side).wait_recv()
         hi, lo = split(sm_in[side])
         sn_hi[side] = hi
         sn_lo[side] = lo
-        for k in range(LEV):
-            hi, lo = split(first[k].reshape(PTS, Q))
-            taken = dot3(nb_hi[k, side], nb_lo[k, side], hi, lo)
-            hi, lo = split(taken)
-            corr[k, side] = dot3(sn_hi[side], sn_lo[side], hi, lo)
-
-    def second_from(k, side, last):
+
+    def correct(k, side):
+        hi, lo = split(first[k].reshape(PTS, Q))
+        taken = dot3(nb_hi[k, side], nb_lo[k, side], hi, lo)
+        hi, lo = split(taken)
+        corr[k, side] = dot3(sn_hi[side], sn_lo[side], hi, lo)
+
+    def second_from(k, side, start):
         ex2(k, side).wait_recv()
         part = mix(k, 2 * side, f2[k, side])
         here = base[k]
@@ -323,11 +323,11 @@
         once[k, side] = terms[:64]
         twice_own[k, side] = terms[64:]
         ex_p(k, side).start()
-        if last:
-            hi, lo = split(total[k] + part)
-            total[k] = dot3(h_hi[...], h_lo[...], hi, lo)
-        else:
-            total[k] = here + part
+        total[k] = (here if start else total[k]) + part
+
+    def settle(k):
+        hi, lo = split(total[k])
+        total[k] = dot3(h_hi[...], h_lo[...], hi, lo)
 
     def relay(k, side):
         ex_p(k, side).wait_recv()
@@ -350,32 +350,37 @@
         @pl.when(edge)
         def _():
             if k >= 1:
-                second_from(k - 1, near, False)
+                second_from(k - 1, near, True)
+            if k == 1:
+                meet(near)
             if k == 2:
-                neighbour_matrices(near)
+                correct(0, near)
+            if k >= 2:
+                correct(k - 1, near)
+                relay(k - 2, near)
 
     @pl.when(edge)
     def _():
-        second_from(LEV - 1, near, False)
+        second_from(LEV - 1, near, True)
+        correct(LEV - 1, near)
+        for k in (LEV - 2, LEV - 1):
+            relay(k, near)
 
     @pl.when(jnp.logical_not(edge))
     def _():
         hand_matrices()
         for k in range(LEV):
-            second_from(k, near, False)
-        neighbour_matrices(near)
-
-    corrections(near)
-
-    @pl.when(jnp.logical_not(middle))
-    def _():
-        for k in range(LEV):
+            second_from(k, ahead, True)
+        for k in range(LEV):
+            second_from(k, 1 - ahead, False)
+        meet(near)
+        for k in range(LEV):
+            correct(k, near)
             relay(k, near)
 
-    neighbour_matrices(far)
-    corrections(far)
-    for side in range(2):
-        ex_v(side).wait_recv()
+    meet(far)
+    for k in range(LEV):
+        correct(k, far)
     from_prev, from_next = v_in[0], v_in[1]
     none = jnp.zeros((64, 64), F32)
     blocks = jnp.concatenate(
@@ -391,31 +396,35 @@
     h_lo[...] = lo
 
     def finish(k):
+        wait_bytes(twice_in.at[k], recvq.at[k])
         for side in range(2):
-            ex_q(k, side).wait_recv()
             terms_in[k, side, pl.ds(64, 64)] = twice_in[k, side] + corr[k, side, pl.ds(64, 64)]
         hi, lo = split(terms_in[k].reshape(PTS, Q))
         outbuf[:, k] = cube(total[k] + dot3(e_hi[...], e_lo[...], hi, lo))
 
-    for j in range(LEV + 1):
-        if j < LEV:
-            second_from(j, far, True)
-        if j >= 1:
-            relay(j - 1, far)
-
-            @pl.when(middle)
-            def _():
-                relay(j - 1, near)
-
-    for k in range(LEV):
-        finish(k)
+    @pl.when(edge)
+    def _():
+        for j in range(LEV + 1):
+            if j < LEV:
+                second_from(j, far, False)
+            if j >= 1:
+                relay(j - 1, far)
+                settle(j - 1)
+        for k in range(LEV - 1):
+            finish(k)
+
+    @pl.when(jnp.logical_not(edge))
+    def _():
+        for k in range(LEV):
+            settle(k)
+        for k in range(LEV):
+            relay(k, far)
+        for k in range(LEV - 1):
+            finish(k)
+
+    finish(LEV - 1)
     for side in range(2):
-        ex_w(side).wait_send()
-        ex_v(side).wait_send()
-        ex_s(side).wait_send()
-        for k in range(LEV):
-            for send in (ex1, ex2, ex_p, ex_q):
-                send(k, side).wait_send()
+        wait_bytes(w_hi, sent.at[side])
 
 
 def local(tracers, sources, weights, dep_owner, dep_slot, nbr_elem, nbr_edge, metric):
@@ -442,9 +451,8 @@
         vmem((LEV, 2, 128, Q), F32),
         vmem((PTS, PTS), BF16), vmem((PTS, PTS), BF16),
         vmem((PTS, PTS), BF16), vmem((PTS, PTS), BF16),
-        dma((6,)), dma((2, LEV)),
-        dma((LEV, 2)), dma((LEV, 2)), dma((LEV, 2)), dma((LEV, 2)), dma((3, 2)), dma((3, 2)),
-        dma((LEV, 2)), dma((LEV, 2)), dma((LEV, 2)), dma((LEV, 2)),
+        dma((6,)), dma((2,)),
+        dma((2,)), dma((LEV, 2)), dma((LEV, 2)), dma((2,)), dma((LEV, 2)), dma((LEV,)),
     ]
     return pl.pallas_call(
         functools.partial(kernel, count),

time: 32.2 us -> 31.1 us (0.966)
  the two profiles are of different devices: /device:TPU:67 before, /device:TPU:1 now
where the time goes in v4:
time: 31.1 us; the launch traced here: 31 us
  Pallas kernels  30.2 us (97%)
  local copies, waits for them, and re-layouts  0.8 us (3%)
    pallas_call x1, Pallas kernels, local(): pl.pallas_call(functools.partial(kernel, count), out_shape=pltpu.VMEM(tra...  30.2 us
    unnamed x1, local copies, waits for them, and re-layouts  0.8 us

profile of v4, /device:TPU:1, one launch (start us, length us, event | category | flops | bytes accessed | tf_op | source)
XLA Modules:
  0.0 31.0 jit_solution(8866407765694447925)
XLA Ops:
  0.0 30.2 %tracer_step.1 = f32[16,4,16,128]{3,2,1,0:T(8,128)S(1)} custom-call(f32[16,4,16,128]{3,2,1,0:T(8,128)} %tracers.1, f32[16,4,16,128]{3,2,1,0:T(8,128)} %sources.1, f32[16,4,256]{2,1,0:T(4,128)} %weights.1, s32[16,4,16]{2,1,0:T(4,128)} %dep_owner.1, s32[16,4,16]{2,1,0:T(4,128)} %dep_slot.1, s32[4,16]{1,0:T(4,128)} %bitcast.2, s32[4,16]{1,0:T(4,128)} %bitcast.3, ...), custom_call_target="tpu_custom_call" | custom-call | tf_op jit(solution)/shard_map/tracer_step/pallas_call | solution.py:457
  30.2 0.8 %copy.10 = f32[16,4,16,128]{3,2,1,0:T(8,128)} copy(f32[16,4,16,128]{3,2,1,0:T(8,128)S(1)} %tracer_step.1) | data formatting | bytes 1048576

commit v5 on v4

--- a/solution.py
+++ b/solution.py
@@ -90,11 +90,11 @@
     tracers, sources, weights, dep_owner, dep_slot, nbr_elem, nbr_edge, metric,
     outbuf,
     own_t, src, wx, dow, dsl, nel, ned, met,
-    f1, first, f2, base, total,
-    w_hi, w_lo, wx_in, nb_hi, nb_lo,
-    v_out, v_in, sm, sm_hi, sm_lo, sm_in, sn_hi, sn_lo,
+    f1, own, partial, first, f2, fix, base, total,
+    w_hi, w_lo, wx_in, nb_hi, nb_lo, taken_hi, taken_lo, span,
+    sm, sm_hi, sm_lo, sm_in, sn_hi, sn_lo,
     corr, vz_hi, vz_lo, once, twice_own, twice, once_in, twice_in, terms_in,
-    h_hi, h_lo, e_hi, e_lo,
+    h_hi, h_lo, e_hi, e_lo, eq_hi, eq_lo, back_hi, back_lo,
     loc, loc_t,
     sent, recv1, recv2, recvm, recvp, recvq,
 ):
@@ -103,6 +103,8 @@
     near = jnp.where(place_in_row < 4, 1, 0)
     far = 1 - near
     edge = (place_in_row == 0) | (place_in_row == 7)
+    twin = jnp.where(lax.rem(me, 2) == 0, 1, 0)
+    remote_side = 1 - twin
     middle = (place_in_row == 3) | (place_in_row == 4)
     ahead = jnp.where(middle, far, near)
 
@@ -142,16 +144,16 @@
         return remote(own_t.at[k], f1.at[k, side], sent.at[side], recv1.at[k, side], side)
 
     def ex2(k, side):
-        return remote(first.at[k], f2.at[k, side], sent.at[side], recv2.at[k, side], side)
+        return remote(partial.at[k, side], f2.at[k, side], sent.at[side], recv2.at[k, side], side)
 
     def ex_w(side):
-        return remote(wx, wx_in.at[side], sent.at[side], recvm.at[side], side)
-
-    def ex_v(side):
-        return remote(v_out.at[side], v_in.at[side], sent.at[side], recvm.at[side], side)
-
-    def ex_s(side):
-        return remote(sm.at[side], sm_in.at[side], sent.at[side], recvm.at[side], side)
+        return remote(wx, wx_in.at[side], sent.at[side], recvm.at[0, side], side)
+
+    def ex_m(side, part):
+        rows_of = pl.ds(64 * part, 64)
+        return remote(
+            sm.at[side, rows_of], sm_in.at[side, rows_of], sent.at[side], recvm.at[1 + part, side], side
+        )
 
     def ex_p(k, side):
         return remote(once.at[k, side], once_in.at[k, side], sent.at[side], recvp.at[k, side], side)
@@ -182,6 +184,8 @@
     for e in range(16):
         code = offset_of(dow[e], me, count) * 16 + dsl[e]
         wx[e, :, pl.ds(PTS, 16)] = code.astype(F32)
+    for side in range(2):
+        ex_w(side).start()
     wait_bytes(src, loc_t.at[1])
     diagonal = (cols((16, PTS)) >> 4) == rows((16, PTS))
     eye16 = cols((16, 16)) == rows((16, 16))
@@ -215,7 +219,7 @@
             match = code == (lane_elem + float(16 * i))
             w_hi[k, i] = jnp.where(match, hi, 0.0).astype(BF16)
             w_lo[k, i] = jnp.where(match, lo, 0.0).astype(BF16)
-        first[k] = cube(mix(k, 1, own_t[k])) + src[k]
+        own[k] = mix(k, 1, own_t[k]) + src[k].reshape(PTS, Q)
 
     square = (PTS, PTS)
     r, c = rows(square), cols(square)
@@ -267,24 +271,20 @@
     picked = dot(pack, spread)
     km = dot_split(picked, m)
     g = dot_split(r_own, m)
-    v = dot_split(km, r_out)
-    v_out[0] = v[:64]
-    v_out[1] = v[64:]
-    for side, through in enumerate((v[:64, :64], v[64:, 64:])):
+    for side, through in enumerate((dot_split(km[:64], r_out[:, :64]), dot_split(km[64:], r_out[:, 64:]))):
         hi, lo = split(through)
         vz_hi[side] = hi
         vz_lo[side] = lo
+    lands = ((off != 1) & (c == pe * 4 + 3 - point)).astype(F32).astype(BF16)
+    landed = dot(pack, lands).T.astype(BF16)
+    r_nb = dot(spread_t, landed) / counts
+    for side, back in enumerate((dot_split(r_nb[:, 64:], km[64:]), dot_split(r_nb[:, :64], km[:64]))):
+        hi, lo = split(back)
+        back_hi[side] = hi
+        back_lo[side] = lo
     kmg = dot_split(km, g)
     sm[0] = jnp.concatenate([km[:64], kmg[:64]], axis=0)
     sm[1] = jnp.concatenate([km[64:], kmg[64:]], axis=0)
-
-    def hand_matrices():
-        for side in range(2):
-            ex_w(side).start()
-            ex_s(side).start()
-            ex_v(side).start()
-
-    pl.when(edge)(hand_matrices)
     for side in range(2):
         hi, lo = split(sm[side])
         sm_hi[side] = hi
@@ -295,28 +295,51 @@
     hi, lo = split(ext)
     e_hi[...] = hi
     e_lo[...] = lo
+    for side in range(2):
+        hi, lo = split(-VISCOSITY * r_out[:, 64 * side : 64 * side + 64])
+        eq_hi[side] = hi
+        eq_lo[side] = lo
 
     def meet(side):
-        wait_bytes(first.at[pl.ds(0, 2)], recvm.at[side])
+        ex_w(side).wait_recv()
         shift = jnp.where(side == 0, 32.0, 0.0)
         for k in range(LEV):
             hi, lo, code = tiled(wx_in.at[side], k)
             match = code == (lane_elem + shift)
-            nb_hi[k, side] = jnp.where(match, hi, 0.0).astype(BF16)
-            nb_lo[k, side] = jnp.where(match, lo, 0.0).astype(BF16)
-        hi, lo = split(sm_in[side])
-        sn_hi[side] = hi
-        sn_lo[side] = lo
-
-    def correct(k, side):
-        hi, lo = split(first[k].reshape(PTS, Q))
-        taken = dot3(nb_hi[k, side], nb_lo[k, side], hi, lo)
-        hi, lo = split(taken)
-        corr[k, side] = dot3(sn_hi[side], sn_lo[side], hi, lo)
+            n_hi = jnp.where(match, hi, 0.0).astype(BF16)
+            n_lo = jnp.where(match, lo, 0.0).astype(BF16)
+            nb_hi[k, side] = n_hi
+            nb_lo[k, side] = n_lo
+            hi, lo = split(own_t[k].reshape(PTS, Q))
+            fix[k, side] = dot3(n_hi, n_lo, hi, lo)
+
+    def matrix_in(side, part):
+        ex_m(side, part).wait_recv()
+        hi, lo = split(sm_in[side, pl.ds(64 * part, 64)])
+        sn_hi[side, part] = hi
+        sn_lo[side, part] = lo
+
+    def take(k, side):
+        hi, lo = split(first[k])
+        hi, lo = split(dot3(nb_hi[k, side], nb_lo[k, side], hi, lo))
+        taken_hi[k, side] = hi
+        taken_lo[k, side] = lo
+
+    def correct_once(k, side):
+        corr[k, side, pl.ds(0, 64)] = dot3(
+            sn_hi[side, 0], sn_lo[side, 0], taken_hi[k, side], taken_lo[k, side]
+        )
+
+    def correct_twice(side):
+        matrix_in(side, 1)
+        for k in range(LEV):
+            corr[k, side, pl.ds(64, 64)] = dot3(
+                sn_hi[side, 1], sn_lo[side, 1], taken_hi[k, side], taken_lo[k, side]
+            )
 
     def second_from(k, side, start):
         ex2(k, side).wait_recv()
-        part = mix(k, 2 * side, f2[k, side])
+        part = mix(k, 2 * side, f2[k, side].reshape(PTS, Q) + fix[k, side])
         here = base[k]
         hi, lo = split(here + part)
         terms = dot3(sm_hi[side], sm_lo[side], hi, lo)
@@ -337,14 +360,23 @@
         twice[k, side] = twice_own[k, side] + dot3(vz_hi[side], vz_lo[side], hi, lo)
         ex_q(k, side).start()
 
+    meet(twin)
     for k in range(LEV):
-        value = first[k].reshape(PTS, Q)
-        for side in range(2):
-            ex1(k, side).wait_recv()
-            value = value + mix(k, 2 * side, f1[k, side])
-        first[k] = cube(value)
-        for side in range(2):
-            ex2(k, side).start()
+        ex1(k, twin).wait_recv()
+        value = own[k] + mix(k, 2 * twin, f1[k, twin])
+        partial[k, twin] = cube(value)
+        ex2(k, twin).start()
+        first[k] = value
+    for side in range(2):
+        ex_m(side, 0).start()
+
+    for k in range(LEV):
+        ex1(k, remote_side).wait_recv()
+        part = mix(k, 2 * remote_side, f1[k, remote_side])
+        partial[k, remote_side] = cube(own[k] + part)
+        ex2(k, remote_side).start()
+        value = first[k] + part
+        first[k] = value
         base[k] = mix(k, 1, value) + src[k].reshape(PTS, Q)
 
         @pl.when(edge)
@@ -352,79 +384,93 @@
             if k >= 1:
                 second_from(k - 1, near, True)
             if k == 1:
-                meet(near)
+                matrix_in(near, 0)
             if k == 2:
-                correct(0, near)
+                take(0, near)
+                correct_once(0, near)
             if k >= 2:
-                correct(k - 1, near)
+                take(k - 1, near)
+                correct_once(k - 1, near)
                 relay(k - 2, near)
 
     @pl.when(edge)
     def _():
         second_from(LEV - 1, near, True)
-        correct(LEV - 1, near)
+        take(LEV - 1, near)
+        correct_once(LEV - 1, near)
         for k in (LEV - 2, LEV - 1):
             relay(k, near)
+        for side in range(2):
+            ex_m(side, 1).start()
+
+    meet(remote_side)
 
     @pl.when(jnp.logical_not(edge))
     def _():
-        hand_matrices()
         for k in range(LEV):
             second_from(k, ahead, True)
         for k in range(LEV):
             second_from(k, 1 - ahead, False)
-        meet(near)
-        for k in range(LEV):
-            correct(k, near)
+        for k in range(LEV):
+            take(k, near)
+            take(k, far)
+        matrix_in(near, 0)
+        for k in range(LEV):
+            correct_once(k, near)
             relay(k, near)
-
-    meet(far)
+        for side in range(2):
+            ex_m(side, 1).start()
+
+    @pl.when(edge)
+    def _():
+        for k in range(LEV):
+            second_from(k, far, False)
+            take(k, far)
+
+    matrix_in(far, 0)
     for k in range(LEV):
-        correct(k, far)
-    from_prev, from_next = v_in[0], v_in[1]
-    none = jnp.zeros((64, 64), F32)
-    blocks = jnp.concatenate(
-        [
-            jnp.concatenate([none, from_prev[:, 64:]], axis=1),
-            jnp.concatenate([from_next[:, :64], none], axis=1),
-        ],
-        axis=0,
+        correct_once(k, far)
+    for k in range(LEV - 1):
+        relay(k, far)
+    through = jnp.concatenate(
+        [dot3(sn_hi[side, 0], sn_lo[side, 0], back_hi[side], back_lo[side]) for side in range(2)], axis=0
     )
-    h = jnp.where(unit, 1.0, 0.0) - VISCOSITY * (gg + dot_split(dot_split(r_out, blocks), km))
+    h = jnp.where(unit, 1.0, 0.0) - VISCOSITY * (gg + dot_split(r_out, through))
     hi, lo = split(h)
     h_hi[...] = hi
     h_lo[...] = lo
 
-    def finish(k):
+    relay(LEV - 1, far)
+    for k in range(LEV):
+        settle(k)
+    correct_twice(near)
+
+    def gather(k, whole):
         wait_bytes(twice_in.at[k], recvq.at[k])
         for side in range(2):
-            terms_in[k, side, pl.ds(64, 64)] = twice_in[k, side] + corr[k, side, pl.ds(64, 64)]
+            terms_in[k, side, pl.ds(64, 64)] = twice_in[k, side] + jnp.where(
+                whole | (side == near), corr[k, side, pl.ds(64, 64)], 0.0
+            )
         hi, lo = split(terms_in[k].reshape(PTS, Q))
-        outbuf[:, k] = cube(total[k] + dot3(e_hi[...], e_lo[...], hi, lo))
+        return total[k] + dot3(e_hi[...], e_lo[...], hi, lo)
 
     @pl.when(edge)
     def _():
-        for j in range(LEV + 1):
-            if j < LEV:
-                second_from(j, far, False)
-            if j >= 1:
-                relay(j - 1, far)
-                settle(j - 1)
-        for k in range(LEV - 1):
-            finish(k)
+        for k in range(LEV):
+            total[k] = gather(k, False)
+        correct_twice(far)
+        for k in range(LEV):
+            hi, lo = split(corr[k, far, pl.ds(64, 64)])
+            outbuf[:, k] = cube(total[k] + dot3(eq_hi[far], eq_lo[far], hi, lo))
 
     @pl.when(jnp.logical_not(edge))
     def _():
-        for k in range(LEV):
-            settle(k)
-        for k in range(LEV):
-            relay(k, far)
-        for k in range(LEV - 1):
-            finish(k)
-
-    finish(LEV - 1)
+        correct_twice(far)
+        for k in range(LEV):
+            outbuf[:, k] = cube(gather(k, True))
+
     for side in range(2):
-        wait_bytes(w_hi, sent.at[side])
+        wait_bytes(span, sent.at[side])
 
 
 def local(tracers, sources, weights, dep_owner, dep_slot, nbr_elem, nbr_edge, metric):
@@ -440,19 +486,22 @@
         vmem(block, F32), vmem(block, F32), vmem((16, LEV, 384), F32),
         vmem(dep_owner.shape, I32), vmem(dep_slot.shape, I32),
         vmem(nbr_elem.shape[::-1], I32), vmem(nbr_edge.shape[::-1], I32), vmem(metric.shape, F32),
-        vmem(pairs, F32), vmem(block, F32), vmem(pairs, F32), vmem(flat, F32), vmem(flat, F32),
+        vmem(pairs, F32), vmem(flat, F32), vmem(pairs, F32), vmem(flat, F32),
+        vmem(pairs, F32), vmem((LEV, 2, PTS, Q), F32), vmem(flat, F32), vmem(flat, F32),
         vmem((LEV, 3, PTS, PTS), BF16), vmem((LEV, 3, PTS, PTS), BF16),
         vmem((2, 16, LEV, 384), F32), vmem((LEV, 2, PTS, PTS), BF16), vmem((LEV, 2, PTS, PTS), BF16),
-        vmem((2, 64, 128), F32), vmem((2, 64, 128), F32),
+        vmem((LEV, 2, PTS, Q), BF16), vmem((LEV, 2, PTS, Q), BF16), vmem((47, 64, 128), F32),
         vmem(tall, F32), vmem(tall, BF16), vmem(tall, BF16),
-        vmem(tall, F32), vmem(tall, BF16), vmem(tall, BF16),
+        vmem(tall, F32), vmem((2, 2, 64, PTS), BF16), vmem((2, 2, 64, PTS), BF16),
         vmem((LEV, 2, 128, Q), F32), vmem((2, 64, 64), BF16), vmem((2, 64, 64), BF16),
         vmem(slim, F32), vmem(slim, F32), vmem(slim, F32), vmem(slim, F32), vmem(slim, F32),
         vmem((LEV, 2, 128, Q), F32),
         vmem((PTS, PTS), BF16), vmem((PTS, PTS), BF16),
         vmem((PTS, PTS), BF16), vmem((PTS, PTS), BF16),
+        vmem((2, PTS, 64), BF16), vmem((2, PTS, 64), BF16),
+        vmem((2, PTS, PTS), BF16), vmem((2, PTS, PTS), BF16),
         dma((6,)), dma((2,)),
-        dma((2,)), dma((LEV, 2)), dma((LEV, 2)), dma((2,)), dma((LEV, 2)), dma((LEV,)),
+        dma((2,)), dma((LEV, 2)), dma((LEV, 2)), dma((3, 2)), dma((LEV, 2)), dma((LEV,)),
     ]
     return pl.pallas_call(
         functools.partial(kernel, count),

time: 31.1 us -> 29.7 us (0.955)
  Pallas kernels: 30.2 us -> 28.8 us
    pallas_call x1, Pallas kernels: 30.2 us -> 28.8 us  [local(): pl.pallas_call(functools.partial(kernel, count), out_shape=pltpu.VMEM(tra...]
where the time goes in v5:
time: 29.7 us; the launch traced here: 29.6 us
  Pallas kernels  28.8 us (97%)
  local copies, waits for them, and re-layouts  0.8 us (3%)
    pallas_call x1, Pallas kernels, local(): pl.pallas_call(functools.partial(kernel, count), out_shape=pltpu.VMEM(tra...  28.8 us
    unnamed x1, local copies, waits for them, and re-layouts  0.8 us

profile of v5, /device:TPU:1, one launch (start us, length us, event | category | flops | bytes accessed | tf_op | source)
XLA Modules:
  0.0 29.6 jit_solution(5044649148366805141)
XLA Ops:
  0.0 28.8 %tracer_step.1 = f32[16,4,16,128]{3,2,1,0:T(8,128)S(1)} custom-call(f32[16,4,16,128]{3,2,1,0:T(8,128)} %tracers.1, f32[16,4,16,128]{3,2,1,0:T(8,128)} %sources.1, f32[16,4,256]{2,1,0:T(4,128)} %weights.1, s32[16,4,16]{2,1,0:T(4,128)} %dep_owner.1, s32[16,4,16]{2,1,0:T(4,128)} %dep_slot.1, s32[4,16]{1,0:T(4,128)} %bitcast.2, s32[4,16]{1,0:T(4,128)} %bitcast.3, ...), custom_call_target="tpu_custom_call" | custom-call | tf_op jit(solution)/shard_map/tracer_step/pallas_call | solution.py:506
  28.8 0.8 %copy.10 = f32[16,4,16,128]{3,2,1,0:T(8,128)} copy(f32[16,4,16,128]{3,2,1,0:T(8,128)S(1)} %tracer_step.1) | data formatting | bytes 1048576

commit v6 on v5

--- a/solution.py
+++ b/solution.py
@@ -89,12 +89,12 @@
     count,
     tracers, sources, weights, dep_owner, dep_slot, nbr_elem, nbr_edge, metric,
     outbuf,
-    own_t, src, wx, dow, dsl, nel, ned, met,
+    own_t, src, wx, cd, cd_in, dow, dsl, nel, ned, met,
     f1, own, partial, first, f2, fix, base, total,
     w_hi, w_lo, wx_in, nb_hi, nb_lo, taken_hi, taken_lo, span,
-    sm, sm_hi, sm_lo, sm_in, sn_hi, sn_lo,
+    km_cut, km_in, km_twice, km_twice_in, mine, sm_hi, sm_lo, sn_hi, sn_lo,
     corr, vz_hi, vz_lo, once, twice_own, twice, once_in, twice_in, terms_in,
-    h_hi, h_lo, e_hi, e_lo, eq_hi, eq_lo, back_hi, back_lo,
+    h_hi, h_lo, e_hi, e_lo, back_hi, back_lo,
     loc, loc_t,
     sent, recv1, recv2, recvm, recvp, recvq,
 ):
@@ -125,7 +125,7 @@
         pltpu.make_async_copy(a, b, loc.at[i])
         for i, (a, b) in enumerate(
             [
-                (weights, wx.at[:, :, pl.ds(0, PTS)]),
+                (weights, wx),
                 (dep_owner, dow),
                 (dep_slot, dsl),
                 (nbr_elem, nel),
@@ -134,8 +134,8 @@
             ]
         )
     ]
-    load_t = [pltpu.make_async_copy(tracers.at[:, k], own_t.at[k], loc_t.at[0]) for k in range(LEV)]
-    load_s = [pltpu.make_async_copy(sources.at[:, k], src.at[k], loc_t.at[1]) for k in range(LEV)]
+    load_t = [pltpu.make_async_copy(tracers.at[:, k], own_t.at[k], loc_t.at[1 + k]) for k in range(LEV)]
+    load_s = [pltpu.make_async_copy(sources.at[:, k], src.at[k], loc_t.at[0]) for k in range(LEV)]
 
     def wait_bytes(like, semaphore):
         pltpu.make_async_copy(like, like, semaphore).wait()
@@ -149,10 +149,13 @@
     def ex_w(side):
         return remote(wx, wx_in.at[side], sent.at[side], recvm.at[0, side], side)
 
+    def ex_c(side):
+        return remote(cd, cd_in.at[side], sent.at[side], recvm.at[3, side], side)
+
     def ex_m(side, part):
-        rows_of = pl.ds(64 * part, 64)
+        ends = ((km_cut, km_in), (km_twice, km_twice_in))[part]
         return remote(
-            sm.at[side, rows_of], sm_in.at[side, rows_of], sent.at[side], recvm.at[1 + part, side], side
+            ends[0].at[side], ends[1].at[side], sent.at[side], recvm.at[1 + part, side], side
         )
 
     def ex_p(k, side):
@@ -172,34 +175,36 @@
         c.start()
     for c in load_s:
         c.start()
-    wait_bytes(own_t, loc_t.at[0])
     pl.semaphore_wait(barrier, 2)
     for k in range(LEV):
+        load_t[k].wait()
         for side in range(2):
             ex1(k, side).start()
 
     for c in small:
         c.wait()
-    wx[:, :, pl.ds(PTS, 128)] = jnp.zeros((16, LEV, 128), F32)
+    cd[...] = jnp.zeros((16, 128), F32)
     for e in range(16):
-        code = offset_of(dow[e], me, count) * 16 + dsl[e]
-        wx[e, :, pl.ds(PTS, 16)] = code.astype(F32)
+        code = (offset_of(dow[e], me, count) * 16 + dsl[e]).astype(F32)
+        for k in range(LEV):
+            cd[pl.ds(e, 1), pl.ds(16 * k, 16)] = code[k : k + 1]
     for side in range(2):
         ex_w(side).start()
-    wait_bytes(src, loc_t.at[1])
+        ex_c(side).start()
+    wait_bytes(src, loc_t.at[0])
     diagonal = (cols((16, PTS)) >> 4) == rows((16, PTS))
     eye16 = cols((16, 16)) == rows((16, 16))
     tile_j = ((rows((PTS, PTS)) & 15) == (cols((PTS, PTS)) & 15)).astype(F32).astype(BF16)
     lane_elem = (cols((1, PTS)) >> 4).astype(F32)
 
-    def tiled(table, k):
+    def tiled(table, marks, k):
         his, los, codes = [], [], []
         for e in range(16):
-            row = table[e, pl.ds(k, 1), pl.ds(0, PTS)]
+            row = table[e, pl.ds(k, 1), :]
             hi = row.astype(BF16).astype(F32)
             his.append(jnp.where(diagonal, jnp.broadcast_to(hi, (16, PTS)), 0.0))
             los.append(jnp.where(diagonal, jnp.broadcast_to(row - hi, (16, PTS)), 0.0))
-            code = table[e, pl.ds(k, 1), pl.ds(PTS, 16)]
+            code = marks[pl.ds(e, 1), pl.ds(16 * k, 16)]
             codes.append(jnp.where(eye16, jnp.broadcast_to(code, (16, 16)), 0.0))
         hi = dot(jnp.concatenate(his, axis=0).astype(BF16), tile_j)
         lo = dot(jnp.concatenate(los, axis=0).astype(BF16), tile_j)
@@ -214,7 +219,7 @@
         return x.reshape(16, 16, Q)
 
     for k in range(LEV):
-        hi, lo, code = tiled(wx, k)
+        hi, lo, code = tiled(wx, cd, k)
         for i in range(3):
             match = code == (lane_elem + float(16 * i))
             w_hi[k, i] = jnp.where(match, hi, 0.0).astype(BF16)
@@ -283,10 +288,23 @@
         back_hi[side] = hi
         back_lo[side] = lo
     kmg = dot_split(km, g)
-    sm[0] = jnp.concatenate([km[:64], kmg[:64]], axis=0)
-    sm[1] = jnp.concatenate([km[64:], kmg[64:]], axis=0)
+    fold = ((rows((PTS, 128)) & 15) == cols((PTS, 128))).astype(F32)
+    cut = dot_split(km, fold)
     for side in range(2):
-        hi, lo = split(sm[side])
+        km_cut[side] = cut[64 * side : 64 * side + 64]
+        km_twice[side] = kmg[64 * side : 64 * side + 64]
+    unfold = (rows((128, PTS)) == (cols((128, PTS)) & 15)).astype(F32).astype(BF16)
+    place_pe = jnp.where(off == 1, -1, jnp.where(off == 2, 0, 64) + rank_pe * 4 + point)
+    arrive = (cols((PTS, 128)) == place_pe).astype(F32).T.astype(BF16)
+    facing = dot(dot(arrive, lands).astype(BF16), same_elem.astype(F32).astype(BF16))
+    mine[1] = (facing[:64] > 0.5).astype(F32)
+    mine[0] = (facing[64:] > 0.5).astype(F32)
+    for side in range(2):
+        hi, lo = split(
+            jnp.concatenate(
+                [km[64 * side : 64 * side + 64], kmg[64 * side : 64 * side + 64]], axis=0
+            )
+        )
         sm_hi[side] = hi
         sm_lo[side] = lo
     gr = dot_split(g, r_out)
@@ -295,16 +313,13 @@
     hi, lo = split(ext)
     e_hi[...] = hi
     e_lo[...] = lo
-    for side in range(2):
-        hi, lo = split(-VISCOSITY * r_out[:, 64 * side : 64 * side + 64])
-        eq_hi[side] = hi
-        eq_lo[side] = lo
 
     def meet(side):
         ex_w(side).wait_recv()
+        ex_c(side).wait_recv()
         shift = jnp.where(side == 0, 32.0, 0.0)
         for k in range(LEV):
-            hi, lo, code = tiled(wx_in.at[side], k)
+            hi, lo, code = tiled(wx_in.at[side], cd_in.at[side], k)
             match = code == (lane_elem + shift)
             n_hi = jnp.where(match, hi, 0.0).astype(BF16)
             n_lo = jnp.where(match, lo, 0.0).astype(BF16)
@@ -315,7 +330,11 @@
 
     def matrix_in(side, part):
         ex_m(side, part).wait_recv()
-        hi, lo = split(sm_in[side, pl.ds(64 * part, 64)])
+        if part == 0:
+            hi, lo = split(km_in[side])
+            hi, lo = split((dot(hi, unfold) + dot(lo, unfold)) * mine[side])
+        else:
+            hi, lo = split(km_twice_in[side])
         sn_hi[side, part] = hi
         sn_lo[side, part] = lo
 
@@ -367,8 +386,9 @@
         partial[k, twin] = cube(value)
         ex2(k, twin).start()
         first[k] = value
-    for side in range(2):
-        ex_m(side, 0).start()
+    for part in range(2):
+        for side in range(2):
+            ex_m(side, part).start()
 
     for k in range(LEV):
         ex1(k, remote_side).wait_recv()
@@ -381,27 +401,19 @@
 
         @pl.when(edge)
         def _():
-            if k >= 1:
-                second_from(k - 1, near, True)
+            second_from(k, near, True)
             if k == 1:
                 matrix_in(near, 0)
-            if k == 2:
-                take(0, near)
-                correct_once(0, near)
-            if k >= 2:
+            if k >= 1:
                 take(k - 1, near)
                 correct_once(k - 1, near)
-                relay(k - 2, near)
 
     @pl.when(edge)
     def _():
-        second_from(LEV - 1, near, True)
         take(LEV - 1, near)
         correct_once(LEV - 1, near)
-        for k in (LEV - 2, LEV - 1):
+        for k in range(LEV):
             relay(k, near)
-        for side in range(2):
-            ex_m(side, 1).start()
 
     meet(remote_side)
 
@@ -418,8 +430,6 @@
         for k in range(LEV):
             correct_once(k, near)
             relay(k, near)
-        for side in range(2):
-            ex_m(side, 1).start()
 
     @pl.when(edge)
     def _():
@@ -445,29 +455,13 @@
         settle(k)
     correct_twice(near)
 
-    def gather(k, whole):
+    correct_twice(far)
+    for k in range(LEV):
         wait_bytes(twice_in.at[k], recvq.at[k])
         for side in range(2):
-            terms_in[k, side, pl.ds(64, 64)] = twice_in[k, side] + jnp.where(
-                whole | (side == near), corr[k, side, pl.ds(64, 64)], 0.0
-            )
+            terms_in[k, side, pl.ds(64, 64)] = twice_in[k, side] + corr[k, side, pl.ds(64, 64)]
         hi, lo = split(terms_in[k].reshape(PTS, Q))
-        return total[k] + dot3(e_hi[...], e_lo[...], hi, lo)
-
-    @pl.when(edge)
-    def _():
-        for k in range(LEV):
-            total[k] = gather(k, False)
-        correct_twice(far)
-        for k in range(LEV):
-            hi, lo = split(corr[k, far, pl.ds(64, 64)])
-            outbuf[:, k] = cube(total[k] + dot3(eq_hi[far], eq_lo[far], hi, lo))
-
-    @pl.when(jnp.logical_not(edge))
-    def _():
-        correct_twice(far)
-        for k in range(LEV):
-            outbuf[:, k] = cube(gather(k, True))
+        outbuf[:, k] = cube(total[k] + dot3(e_hi[...], e_lo[...], hi, lo))
 
     for side in range(2):
         wait_bytes(span, sent.at[side])
@@ -483,25 +477,25 @@
     tall = (2, 128, PTS)
     slim = (LEV, 2, 64, Q)
     scratch = [
-        vmem(block, F32), vmem(block, F32), vmem((16, LEV, 384), F32),
-        vmem(dep_owner.shape, I32), vmem(dep_slot.shape, I32),
+        vmem(block, F32), vmem(block, F32), vmem((16, LEV, PTS), F32), vmem((16, 128), F32),
+        vmem((2, 16, 128), F32), vmem(dep_owner.shape, I32), vmem(dep_slot.shape, I32),
         vmem(nbr_elem.shape[::-1], I32), vmem(nbr_edge.shape[::-1], I32), vmem(metric.shape, F32),
         vmem(pairs, F32), vmem(flat, F32), vmem(pairs, F32), vmem(flat, F32),
         vmem(pairs, F32), vmem((LEV, 2, PTS, Q), F32), vmem(flat, F32), vmem(flat, F32),
         vmem((LEV, 3, PTS, PTS), BF16), vmem((LEV, 3, PTS, PTS), BF16),
-        vmem((2, 16, LEV, 384), F32), vmem((LEV, 2, PTS, PTS), BF16), vmem((LEV, 2, PTS, PTS), BF16),
-        vmem((LEV, 2, PTS, Q), BF16), vmem((LEV, 2, PTS, Q), BF16), vmem((47, 64, 128), F32),
-        vmem(tall, F32), vmem(tall, BF16), vmem(tall, BF16),
-        vmem(tall, F32), vmem((2, 2, 64, PTS), BF16), vmem((2, 2, 64, PTS), BF16),
+        vmem((2, 16, LEV, PTS), F32), vmem((LEV, 2, PTS, PTS), BF16), vmem((LEV, 2, PTS, PTS), BF16),
+        vmem((LEV, 2, PTS, Q), BF16), vmem((LEV, 2, PTS, Q), BF16), vmem((181, 16, 128), F32),
+        vmem((2, 64, 128), F32), vmem((2, 64, 128), F32), vmem((2, 64, PTS), F32),
+        vmem((2, 64, PTS), F32), vmem((2, 64, PTS), F32), vmem(tall, BF16), vmem(tall, BF16),
+        vmem((2, 2, 64, PTS), BF16), vmem((2, 2, 64, PTS), BF16),
         vmem((LEV, 2, 128, Q), F32), vmem((2, 64, 64), BF16), vmem((2, 64, 64), BF16),
         vmem(slim, F32), vmem(slim, F32), vmem(slim, F32), vmem(slim, F32), vmem(slim, F32),
         vmem((LEV, 2, 128, Q), F32),
         vmem((PTS, PTS), BF16), vmem((PTS, PTS), BF16),
         vmem((PTS, PTS), BF16), vmem((PTS, PTS), BF16),
-        vmem((2, PTS, 64), BF16), vmem((2, PTS, 64), BF16),
         vmem((2, PTS, PTS), BF16), vmem((2, PTS, PTS), BF16),
-        dma((6,)), dma((2,)),
-        dma((2,)), dma((LEV, 2)), dma((LEV, 2)), dma((3, 2)), dma((LEV, 2)), dma((LEV,)),
+        dma((6,)), dma((1 + LEV,)),
+        dma((2,)), dma((LEV, 2)), dma((LEV, 2)), dma((4, 2)), dma((LEV, 2)), dma((LEV,)),
     ]
     return pl.pallas_call(
         functools.partial(kernel, count),

time: 29.7 us -> 29.1 us (0.980)
  Pallas kernels: 28.8 us -> 28.2 us
    pallas_call x1, Pallas kernels: 28.8 us -> 28.2 us  [local(): pl.pallas_call(functools.partial(kernel, count), out_shape=pltpu.VMEM(tra...]
where the time goes in v6:
time: 29.1 us; the launch traced here: 29 us
  Pallas kernels  28.2 us (97%)
  local copies, waits for them, and re-layouts  0.8 us (3%)
    pallas_call x1, Pallas kernels, local(): pl.pallas_call(functools.partial(kernel, count), out_shape=pltpu.VMEM(tra...  28.2 us
    unnamed x1, local copies, waits for them, and re-layouts  0.8 us

profile of v6, /device:TPU:1, one launch (start us, length us, event | category | flops | bytes accessed | tf_op | source)
XLA Modules:
  0.0 29.0 jit_solution(4350520930320572170)
XLA Ops:
  0.0 28.2 %tracer_step.1 = f32[16,4,16,128]{3,2,1,0:T(8,128)S(1)} custom-call(f32[16,4,16,128]{3,2,1,0:T(8,128)} %tracers.1, f32[16,4,16,128]{3,2,1,0:T(8,128)} %sources.1, f32[16,4,256]{2,1,0:T(4,128)} %weights.1, s32[16,4,16]{2,1,0:T(4,128)} %dep_owner.1, s32[16,4,16]{2,1,0:T(4,128)} %dep_slot.1, s32[4,16]{1,0:T(4,128)} %bitcast.2, s32[4,16]{1,0:T(4,128)} %bitcast.3, ...), custom_call_target="tpu_custom_call" | custom-call | tf_op jit(solution)/shard_map/tracer_step/pallas_call | solution.py:500
  28.2 0.8 %copy.10 = f32[16,4,16,128]{3,2,1,0:T(8,128)} copy(f32[16,4,16,128]{3,2,1,0:T(8,128)S(1)} %tracer_step.1) | data formatting | bytes 1048576

commit v7 on v6

--- a/solution.py
+++ b/solution.py
@@ -175,11 +175,31 @@
         c.start()
     for c in load_s:
         c.start()
-    pl.semaphore_wait(barrier, 2)
-    for k in range(LEV):
-        load_t[k].wait()
+
+    def send_tracers(loaded):
+        pl.semaphore_wait(barrier, 2)
+        for k in range(LEV):
+            if not loaded:
+                load_t[k].wait()
+            for side in range(2):
+                ex1(k, side).start()
+
+    def send_tables():
         for side in range(2):
-            ex1(k, side).start()
+            ex_w(side).start()
+            ex_c(side).start()
+
+    first_of_all = me == 0
+    others = jnp.logical_not(first_of_all)
+
+    @pl.when(others)
+    def _():
+        send_tracers(False)
+
+    @pl.when(first_of_all)
+    def _():
+        for k in range(LEV):
+            load_t[k].wait()
 
     for c in small:
         c.wait()
@@ -188,9 +208,7 @@
         code = (offset_of(dow[e], me, count) * 16 + dsl[e]).astype(F32)
         for k in range(LEV):
             cd[pl.ds(e, 1), pl.ds(16 * k, 16)] = code[k : k + 1]
-    for side in range(2):
-        ex_w(side).start()
-        ex_c(side).start()
+    pl.when(others)(send_tables)
     wait_bytes(src, loc_t.at[0])
     diagonal = (cols((16, PTS)) >> 4) == rows((16, PTS))
     eye16 = cols((16, 16)) == rows((16, 16))
@@ -380,6 +398,12 @@
         ex_q(k, side).start()
 
     meet(twin)
+
+    @pl.when(first_of_all)
+    def _():
+        send_tracers(True)
+        send_tables()
+
     for k in range(LEV):
         ex1(k, twin).wait_recv()
         value = own[k] + mix(k, 2 * twin, f1[k, twin])
@@ -430,6 +454,7 @@
         for k in range(LEV):
             correct_once(k, near)
             relay(k, near)
+    correct_twice(near)
 
     @pl.when(edge)
     def _():
@@ -440,8 +465,6 @@
     matrix_in(far, 0)
     for k in range(LEV):
         correct_once(k, far)
-    for k in range(LEV - 1):
-        relay(k, far)
     through = jnp.concatenate(
         [dot3(sn_hi[side, 0], sn_lo[side, 0], back_hi[side], back_lo[side]) for side in range(2)], axis=0
     )
@@ -450,11 +473,12 @@
     h_hi[...] = hi
     h_lo[...] = lo
 
-    relay(LEV - 1, far)
     for k in range(LEV):
+        relay(k, far)
+        if k % 2 == 0:
+            settle(k // 2)
+    for k in (LEV - 2, LEV - 1):
         settle(k)
-    correct_twice(near)
-
     correct_twice(far)
     for k in range(LEV):
         wait_bytes(twice_in.at[k], recvq.at[k])

time: 29.1 us -> 28.7 us (0.986)
  Pallas kernels: 28.2 us -> 27.8 us
    pallas_call x1, Pallas kernels: 28.2 us -> 27.8 us  [local(): pl.pallas_call(functools.partial(kernel, count), out_shape=pltpu.VMEM(tra...]
where the time goes in v7:
time: 28.7 us; the launch traced here: 28.6 us
  Pallas kernels  27.8 us (97%)
  local copies, waits for them, and re-layouts  0.8 us (3%)
    pallas_call x1, Pallas kernels, local(): pl.pallas_call(functools.partial(kernel, count), out_shape=pltpu.VMEM(tra...  27.8 us
    unnamed x1, local copies, waits for them, and re-layouts  0.8 us

profile of v7, /device:TPU:1, one launch (start us, length us, event | category | flops | bytes accessed | tf_op | source)
XLA Modules:
  0.0 28.6 jit_solution(16094568907082559164)
XLA Ops:
  0.0 27.8 %tracer_step.1 = f32[16,4,16,128]{3,2,1,0:T(8,128)S(1)} custom-call(f32[16,4,16,128]{3,2,1,0:T(8,128)} %tracers.1, f32[16,4,16,128]{3,2,1,0:T(8,128)} %sources.1, f32[16,4,256]{2,1,0:T(4,128)} %weights.1, s32[16,4,16]{2,1,0:T(4,128)} %dep_owner.1, s32[16,4,16]{2,1,0:T(4,128)} %dep_slot.1, s32[4,16]{1,0:T(4,128)} %bitcast.2, s32[4,16]{1,0:T(4,128)} %bitcast.3, ...), custom_call_target="tpu_custom_call" | custom-call | tf_op jit(solution)/shard_map/tracer_step/pallas_call | solution.py:524
  27.8 0.8 %copy.10 = f32[16,4,16,128]{3,2,1,0:T(8,128)} copy(f32[16,4,16,128]{3,2,1,0:T(8,128)S(1)} %tracer_step.1) | data formatting | bytes 1048576

commit v8 on v7

--- a/solution.py
+++ b/solution.py
@@ -410,9 +410,14 @@
         partial[k, twin] = cube(value)
         ex2(k, twin).start()
         first[k] = value
-    for part in range(2):
+    for side in range(2):
+        ex_m(side, 0).start()
+
+    @pl.when(jnp.logical_not(edge))
+    def _():
         for side in range(2):
-            ex_m(side, part).start()
+            ex_m(side, 1).start()
+
 
     for k in range(LEV):
         ex1(k, remote_side).wait_recv()
@@ -434,6 +439,8 @@
 
     @pl.when(edge)
     def _():
+        for side in range(2):
+            ex_m(side, 1).start()
         take(LEV - 1, near)
         correct_once(LEV - 1, near)
         for k in range(LEV):

time: 28.7 us -> 28.7 us (level)
  no operation moved by 1% of the time
where the time goes in v8:
time: 28.7 us; the launch traced here: 28.5 us
  Pallas kernels  27.7 us (97%)
  local copies, waits for them, and re-layouts  0.8 us (3%)
    pallas_call x1, Pallas kernels, local(): pl.pallas_call(functools.partial(kernel, count), out_shape=pltpu.VMEM(tra...  27.7 us
    unnamed x1, local copies, waits for them, and re-layouts  0.8 us

profile of v8, /device:TPU:1, one launch (start us, length us, event | category | flops | bytes accessed | tf_op | source)
XLA Modules:
  0.0 28.5 jit_solution(5280616466500222623)
XLA Ops:
  0.0 27.7 %tracer_step.1 = f32[16,4,16,128]{3,2,1,0:T(8,128)S(1)} custom-call(f32[16,4,16,128]{3,2,1,0:T(8,128)} %tracers.1, f32[16,4,16,128]{3,2,1,0:T(8,128)} %sources.1, f32[16,4,256]{2,1,0:T(4,128)} %weights.1, s32[16,4,16]{2,1,0:T(4,128)} %dep_owner.1, s32[16,4,16]{2,1,0:T(4,128)} %dep_slot.1, s32[4,16]{1,0:T(4,128)} %bitcast.2, s32[4,16]{1,0:T(4,128)} %bitcast.3, ...), custom_call_target="tpu_custom_call" | custom-call | tf_op jit(solution)/shard_map/tracer_step/pallas_call | solution.py:531
  27.7 0.8 %copy.10 = f32[16,4,16,128]{3,2,1,0:T(8,128)} copy(f32[16,4,16,128]{3,2,1,0:T(8,128)S(1)} %tracer_step.1) | data formatting | bytes 1048576
